TPU v7x, 256 devices: a whole 4x4x8 slice. The times are simulated.
256 devices in a mesh: tm: 16 (over x, z_lo, core), space: 16 (over z_hi, y).
Axes of the slice: x: 4, y: 4, z: 8 (z_hi: 4, z_lo: 2; z = z_hi * 2 + z_lo), core: 2. Of those that a mesh axis runs over, the one named last changes fastest.
Arguments:
- state_rhs: float32 [32, 32, 128, 128], P('tm', 'space'), may hold values from -5 to 9
- adjoint_rhs: float32 [32, 32, 128, 128], P('tm', 'space'), may hold values from -5 to 9
- reaction: float32 [32, 128, 128], P('space'), may hold values from 0.01 to 1
Outputs:
- state_out: float32 [32, 32, 128, 128], P('tm', 'space')
- adjoint_out: float32 [32, 32, 128, 128], P('tm', 'space')
All inputs are finite; a program needn't handle non-finite values.
Results may differ from a plain program's by a relative error of at most 0.00021.
Values sent between devices are 32-bit elements; how exact they have to be, the bound alone decides.
A program may use at most 64 MiB of HBM per device.

v0:
```python
import math

import jax
import jax.numpy as jnp
from jax import lax
from jax.sharding import Mesh
from jax.sharding import PartitionSpec as P

STEPS = 32
SWEEPS = 12
TM = ("tm_0", "tm_1", "tm_2")


ALPHA = 0.1
MU = 1.0
BETA = 1.0


def in_one_piece(arrays, axis, split_dim, concat_dim, along):
    ends, at = ([], 0)
    for a in arrays[:-1]:
        at += a.shape[along]
        ends.append(at)
    both = jnp.concatenate(arrays, axis=along)
    return tuple(
        jnp.split(
            lax.all_to_all(both, axis, split_axis=split_dim, concat_axis=concat_dim, tiled=True),
            ends,
            axis=along,
        )
    )


def split_up(x, dim, count):
    lengths = x.shape
    pieces = x.reshape(*lengths[:dim], count, lengths[dim] // count, *lengths[dim + 1 :])
    return jnp.moveaxis(pieces, dim, 0)


def joined_along(pieces, dim):
    lengths = list(pieces.shape[1:])
    lengths[dim] *= pieces.shape[0]
    return jnp.moveaxis(pieces, 0, dim).reshape(lengths)


def moved_by_axis(pieces, axes, turns):
    lengths = [lax.axis_size(a) for a in axes]
    pieces = pieces.reshape(*lengths, *pieces.shape[1:])
    for k in turns:
        pieces = lax.all_to_all(pieces, axes[k], split_axis=k, concat_axis=k, tiled=True)
    return pieces.reshape(-1, *pieces.shape[len(axes) :])


def two_step_exchange(x, groups, turns, split_dim, concat_dim):
    count = lax.axis_size(groups[0]) * lax.axis_size(groups[1])
    pieces = split_up(x, split_dim, count)
    return joined_along(moved_by_axis(pieces, groups, turns), concat_dim)


def padded_2(cells, sides, width):
    for axis, dim in sides:
        count = lax.axis_size(axis)
        ends = count - 1
        head = lax.slice_in_dim(cells, 0, width, axis=dim)
        tail = lax.slice_in_dim(cells, cells.shape[dim] - width, cells.shape[dim], axis=dim)
        cells = jnp.concatenate(
            [
                lax.ppermute(tail, axis, [(i, (i + 1) % count) for i in range(ends)]),
                cells,
                lax.ppermute(head, axis, [((i + 1) % count, i) for i in range(ends)]),
            ],
            axis=dim,
        )
    return cells


def coefficients(reaction, freqs):
    turn = 2.0 * math.pi * freqs.astype(jnp.float32) / STEPS
    rate = math.exp(math.log(ALPHA) / STEPS)
    lam_re = 1.0 - rate * jnp.cos(turn)
    lam_im = rate * jnp.sin(turn)
    shaped = (-1,) + (1,) * reaction.ndim
    d_re = lam_re.reshape(shaped) + MU * (6.0 + reaction)
    d_im = jnp.broadcast_to(lam_im.reshape(shaped), d_re.shape)
    den_re = d_re * d_re - d_im * d_im + BETA * BETA
    den_im = 2.0 * d_re * d_im
    magnitude = den_re * den_re + den_im * den_im
    inv_re = den_re / magnitude
    inv_im = -den_im / magnitude
    return (
        d_re * inv_re - d_im * inv_im,
        d_re * inv_im + d_im * inv_re,
        BETA * inv_re,
        BETA * inv_im,
    )


def block_solve(coefficient, source):
    q_re, q_im, r_re, r_im = coefficient
    y_real = source[..., 0, :, :, :]
    y_imag = source[..., 1, :, :, :]
    p_real = source[..., 2, :, :, :]
    p_imag = source[..., 3, :, :, :]
    new_yre = q_re * y_real - q_im * y_imag + (r_re * p_real - r_im * p_imag)
    new_yim = q_re * y_imag + q_im * y_real + (r_re * p_imag + r_im * p_real)
    new_pre = q_re * p_real - q_im * p_imag - (r_re * y_real - r_im * y_imag)
    new_pim = q_re * p_imag + q_im * p_real - (r_re * y_imag + r_im * y_real)
    return jnp.stack((new_yre, new_yim, new_pre, new_pim), axis=-4)


def neighbour_sum(zpadded):
    inner = zpadded[:, :, 1:-1]
    padded = jnp.pad(inner, ((0, 0), (0, 0), (0, 0), (1, 1), (1, 1)))
    total = zpadded[:, :, 2:] + zpadded[:, :, :-2]
    total = total + padded[:, :, :, 2:, 1:-1] + padded[:, :, :, :-2, 1:-1]
    return total + padded[:, :, :, 1:-1, 2:] + padded[:, :, :, 1:-1, :-2]


def effective(times, reverse):
    if reverse:
        return STEPS - 1 - times
    return times


def forward_table(freqs, times, reverse):
    moment = effective(times, reverse)
    phase = freqs[:, None] * moment[None, :] % STEPS
    angle = 2.0 * math.pi / STEPS * phase.astype(jnp.float32)
    growth = jnp.exp(math.log(ALPHA) * moment.astype(jnp.float32) / STEPS)[None, :]
    table = jnp.stack((jnp.cos(angle) * growth, -jnp.sin(angle) * growth), axis=1)
    return table.reshape(-1, times.shape[0])


def inverse_table(freqs, times, reverse):
    moment = effective(times, reverse)
    phase = moment[:, None] * freqs[None, :] % STEPS
    angle = 2.0 * math.pi / STEPS * phase.astype(jnp.float32)
    shrink = jnp.exp(-math.log(ALPHA) * moment.astype(jnp.float32) / STEPS)[:, None] / STEPS
    table = jnp.stack((jnp.cos(angle) * shrink, -jnp.sin(angle) * shrink), axis=2)
    return table.reshape(times.shape[0], -1)


def forward_pair(state_part, adjoint_part, freqs, times):
    rows = state_part.shape[0]
    state_hat = jnp.dot(
        forward_table(freqs, times, False),
        state_part.reshape(rows, -1),
        precision=lax.Precision.HIGHEST,
    )
    adjoint_hat = jnp.dot(
        forward_table(freqs, times, True),
        adjoint_part.reshape(rows, -1),
        precision=lax.Precision.HIGHEST,
    )
    return (state_hat, adjoint_hat)


def backward_pair(solved, freqs, times):
    count = solved.shape[0]
    slab = solved.shape[2:]
    flat_state = solved[:, 0:2].reshape(2 * count, -1)
    flat_adjoint = solved[:, 2:4].reshape(2 * count, -1)
    state_time = jnp.dot(
        inverse_table(freqs, times, False), flat_state, precision=lax.Precision.HIGHEST
    )
    adjoint_time = jnp.dot(
        inverse_table(freqs, times, True), flat_adjoint, precision=lax.Precision.HIGHEST
    )
    shaped = (times.shape[0],) + slab
    return (state_time.reshape(shaped), adjoint_time.reshape(shaped))


def body(state_rhs, adjoint_rhs, reaction):
    groups = lax.axis_size(TM)
    freq_count = STEPS // groups
    freqs = lax.axis_index(TM) * freq_count + jnp.arange(freq_count, dtype=jnp.int32)
    state_all, adjoint_all = in_one_piece((state_rhs, adjoint_rhs), TM, 2, 0, 1)
    every = jnp.arange(STEPS, dtype=jnp.int32)
    state_hat, adjoint_hat = forward_pair(state_all, adjoint_all, every, every)
    narrow = state_all.shape[1:]
    spread = jnp.concatenate(
        (state_hat.reshape((STEPS, 2) + narrow), adjoint_hat.reshape((STEPS, 2) + narrow)), axis=1
    )
    sources = two_step_exchange(spread, (("tm_0", "tm_1"), "tm_2"), (1, 0), 0, 3)
    coefficient = coefficients(reaction, freqs)
    field = block_solve(coefficient, sources)

    def sweep(sweep_index, current):
        zpadded = padded_2(current, (("space", 2),), 1)
        return block_solve(coefficient, sources + MU * neighbour_sum(zpadded))

    solved = lax.fori_loop(0, SWEEPS - 1, sweep, field)
    by_time = two_step_exchange(solved, (("tm_0", "tm_1"), "tm_2"), (1, 0), 3, 0)
    every = jnp.arange(STEPS, dtype=jnp.int32)
    state_time, adjoint_time = backward_pair(by_time, every, every)
    state_out, adjoint_out = in_one_piece((state_time, adjoint_time), TM, 0, 2, 1)
    return (state_out, adjoint_out)


def solution(mesh):
    split = Mesh(
        mesh.devices.reshape(4, 2, 2, mesh.shape["space"]), ("tm_0", "tm_1", "tm_2", "space")
    )
    placed = (P(TM, "space", None, None), P(TM, "space", None, None), P("space", None, None))
    return jax.shard_map(
        body,
        mesh=split,
        in_specs=placed,
        out_specs=(P(TM, "space", None, None), P(TM, "space", None, None)),
        check_vma=False,
    )
```

profile of v0, /device:TPU:88, one launch (start us, length us, event | category | flops | bytes accessed | tf_op | source)
XLA Modules:
  0.0 451.5 jit_solution(1778864663796750010)
XLA Ops:
  10.0 10.6 %all-to-all-done = f32[2,4,128,128]{3,1,0,2:T(4,128)S(1)} async-done(((f32[2,4,128,128]{3,1,0,2:T(4,128)}), f32[2,4,128,128]{3,1,0,2:T(4,128)S(1)}, u32[]{:S(2)}, u32[]{:S(2)}) %all-to-all-start) | async-done | bytes 524320 | tf_op jit(solution)/shard_map/all_to_all | solution.py:27
  33.0 16.1 %all-to-all-done.2 = f32[8,2,2,4,2,8,128]{6,2,1,5,4,3,0:T(2,128)S(1)} async-done(((f32[8,2,2,4,2,8,128]{6,2,1,5,4,3,0:T(2,128)}), f32[8,2,2,4,2,8,128]{6,2,1,5,4,3,0:T(2,128)S(1)}, u32[]{:S(2)}, u32[]{:S(2)}) %all-to-all-start.2) | async-done | bytes 1048608 | tf_op jit(solution)/shard_map/all_to_all | solution.py:50
  50.0 339.6 %while.14 = (s32[]{:T(128)}, f32[2,4,2,128,128]{4,3,2,1,0:T(8,128)S(1)}, f32[2,4,2,128,128]{4,3,2,1,0:T(8,128)S(1)}, f32[2]{0:T(128)S(1)}, f32[2,128,128]{2,1,0:...) while((s32[]{:T(128)}, ...), condition=%wide.region_1.2_spmd.clone.clone, body=%wide.region_0.1_spmd.clone.clone.sunk | while | flops 6946818 | bytes 15991021 | solution.py:192
  57.2 19.2 %collective-permute-done = f32[2,4,1,128,128]{4,3,2,1,0:T(8,128)} collective-permute-done((f32[2,4,1,128,128]{4,3,2,1,0:T(8,128)S(1)}, f32[2,4,1,128,128]{4,3,2,1,0:T(8,128)}, u32[]{:S(2)}, u32[]{:S(2)}) %collective-permute-start) | collective-permute-done | bytes 524320 | tf_op jit(solution)/shard_map/while/body/eval_jaxpr/ppermute | solution.py:68
  76.4 9.0 %collective-permute-done.1 = f32[2,4,1,128,128]{4,3,2,1,0:T(8,128)} collective-permute-done((f32[2,4,1,128,128]{4,3,2,1,0:T(8,128)S(1)}, f32[2,4,1,128,128]{4,3,2,1,0:T(8,128)}, u32[]{:S(2)}, u32[]{:S(2)}) %collective-permute-start.1) | collective-permute-done | bytes 524320 | tf_op jit(solution)/shard_map/while/body/eval_jaxpr/ppermute | solution.py:70
  94.0 15.7 %collective-permute-done = f32[2,4,1,128,128]{4,3,2,1,0:T(8,128)} collective-permute-done((f32[2,4,1,128,128]{4,3,2,1,0:T(8,128)S(1)}, f32[2,4,1,128,128]{4,3,2,1,0:T(8,128)}, u32[]{:S(2)}, u32[]{:S(2)}) %collective-permute-start) | collective-permute-done | bytes 524320 | tf_op jit(solution)/shard_map/while/body/eval_jaxpr/ppermute | solution.py:68
  109.6 8.2 %collective-permute-done.1 = f32[2,4,1,128,128]{4,3,2,1,0:T(8,128)} collective-permute-done((f32[2,4,1,128,128]{4,3,2,1,0:T(8,128)S(1)}, f32[2,4,1,128,128]{4,3,2,1,0:T(8,128)}, u32[]{:S(2)}, u32[]{:S(2)}) %collective-permute-start.1) | collective-permute-done | bytes 524320 | tf_op jit(solution)/shard_map/while/body/eval_jaxpr/ppermute | solution.py:70
  126.4 14.5 %collective-permute-done = f32[2,4,1,128,128]{4,3,2,1,0:T(8,128)} collective-permute-done((f32[2,4,1,128,128]{4,3,2,1,0:T(8,128)S(1)}, f32[2,4,1,128,128]{4,3,2,1,0:T(8,128)}, u32[]{:S(2)}, u32[]{:S(2)}) %collective-permute-start) | collective-permute-done | bytes 524320 | tf_op jit(solution)/shard_map/while/body/eval_jaxpr/ppermute | solution.py:68
  154.3 9.0 %collective-permute-done = f32[2,4,1,128,128]{4,3,2,1,0:T(8,128)} collective-permute-done((f32[2,4,1,128,128]{4,3,2,1,0:T(8,128)S(1)}, f32[2,4,1,128,128]{4,3,2,1,0:T(8,128)}, u32[]{:S(2)}, u32[]{:S(2)}) %collective-permute-start) | collective-permute-done | bytes 524320 | tf_op jit(solution)/shard_map/while/body/eval_jaxpr/ppermute | solution.py:68
  163.4 8.3 %collective-permute-done.1 = f32[2,4,1,128,128]{4,3,2,1,0:T(8,128)} collective-permute-done((f32[2,4,1,128,128]{4,3,2,1,0:T(8,128)S(1)}, f32[2,4,1,128,128]{4,3,2,1,0:T(8,128)}, u32[]{:S(2)}, u32[]{:S(2)}) %collective-permute-start.1) | collective-permute-done | bytes 524320 | tf_op jit(solution)/shard_map/while/body/eval_jaxpr/ppermute | solution.py:70
  180.3 8.5 %collective-permute-done = f32[2,4,1,128,128]{4,3,2,1,0:T(8,128)} collective-permute-done((f32[2,4,1,128,128]{4,3,2,1,0:T(8,128)S(1)}, f32[2,4,1,128,128]{4,3,2,1,0:T(8,128)}, u32[]{:S(2)}, u32[]{:S(2)}) %collective-permute-start) | collective-permute-done | bytes 524320 | tf_op jit(solution)/shard_map/while/body/eval_jaxpr/ppermute | solution.py:68
  188.7 11.2 %collective-permute-done.1 = f32[2,4,1,128,128]{4,3,2,1,0:T(8,128)} collective-permute-done((f32[2,4,1,128,128]{4,3,2,1,0:T(8,128)S(1)}, f32[2,4,1,128,128]{4,3,2,1,0:T(8,128)}, u32[]{:S(2)}, u32[]{:S(2)}) %collective-permute-start.1) | collective-permute-done | bytes 524320 | tf_op jit(solution)/shard_map/while/body/eval_jaxpr/ppermute | solution.py:70
  208.5 9.9 %collective-permute-done = f32[2,4,1,128,128]{4,3,2,1,0:T(8,128)} collective-permute-done((f32[2,4,1,128,128]{4,3,2,1,0:T(8,128)S(1)}, f32[2,4,1,128,128]{4,3,2,1,0:T(8,128)}, u32[]{:S(2)}, u32[]{:S(2)}) %collective-permute-start) | collective-permute-done | bytes 524320 | tf_op jit(solution)/shard_map/while/body/eval_jaxpr/ppermute | solution.py:68
  218.4 11.1 %collective-permute-done.1 = f32[2,4,1,128,128]{4,3,2,1,0:T(8,128)} collective-permute-done((f32[2,4,1,128,128]{4,3,2,1,0:T(8,128)S(1)}, f32[2,4,1,128,128]{4,3,2,1,0:T(8,128)}, u32[]{:S(2)}, u32[]{:S(2)}) %collective-permute-start.1) | collective-permute-done | bytes 524320 | tf_op jit(solution)/shard_map/while/body/eval_jaxpr/ppermute | solution.py:70
  238.0 9.9 %collective-permute-done = f32[2,4,1,128,128]{4,3,2,1,0:T(8,128)} collective-permute-done((f32[2,4,1,128,128]{4,3,2,1,0:T(8,128)S(1)}, f32[2,4,1,128,128]{4,3,2,1,0:T(8,128)}, u32[]{:S(2)}, u32[]{:S(2)}) %collective-permute-start) | collective-permute-done | bytes 524320 | tf_op jit(solution)/shard_map/while/body/eval_jaxpr/ppermute | solution.py:68
  248.0 10.4 %collective-permute-done.1 = f32[2,4,1,128,128]{4,3,2,1,0:T(8,128)} collective-permute-done((f32[2,4,1,128,128]{4,3,2,1,0:T(8,128)S(1)}, f32[2,4,1,128,128]{4,3,2,1,0:T(8,128)}, u32[]{:S(2)}, u32[]{:S(2)}) %collective-permute-start.1) | collective-permute-done | bytes 524320 | tf_op jit(solution)/shard_map/while/body/eval_jaxpr/ppermute | solution.py:70
  270.4 16.0 %collective-permute-done = f32[2,4,1,128,128]{4,3,2,1,0:T(8,128)} collective-permute-done((f32[2,4,1,128,128]{4,3,2,1,0:T(8,128)S(1)}, f32[2,4,1,128,128]{4,3,2,1,0:T(8,128)}, u32[]{:S(2)}, u32[]{:S(2)}) %collective-permute-start) | collective-permute-done | bytes 524320 | tf_op jit(solution)/shard_map/while/body/eval_jaxpr/ppermute | solution.py:68
  299.8 16.6 %collective-permute-done = f32[2,4,1,128,128]{4,3,2,1,0:T(8,128)} collective-permute-done((f32[2,4,1,128,128]{4,3,2,1,0:T(8,128)S(1)}, f32[2,4,1,128,128]{4,3,2,1,0:T(8,128)}, u32[]{:S(2)}, u32[]{:S(2)}) %collective-permute-start) | collective-permute-done | bytes 524320 | tf_op jit(solution)/shard_map/while/body/eval_jaxpr/ppermute | solution.py:68
  316.4 8.1 %collective-permute-done.1 = f32[2,4,1,128,128]{4,3,2,1,0:T(8,128)} collective-permute-done((f32[2,4,1,128,128]{4,3,2,1,0:T(8,128)S(1)}, f32[2,4,1,128,128]{4,3,2,1,0:T(8,128)}, u32[]{:S(2)}, u32[]{:S(2)}) %collective-permute-start.1) | collective-permute-done | bytes 524320 | tf_op jit(solution)/shard_map/while/body/eval_jaxpr/ppermute | solution.py:70
  333.1 18.9 %collective-permute-done = f32[2,4,1,128,128]{4,3,2,1,0:T(8,128)} collective-permute-done((f32[2,4,1,128,128]{4,3,2,1,0:T(8,128)S(1)}, f32[2,4,1,128,128]{4,3,2,1,0:T(8,128)}, u32[]{:S(2)}, u32[]{:S(2)}) %collective-permute-start) | collective-permute-done | bytes 524320 | tf_op jit(solution)/shard_map/while/body/eval_jaxpr/ppermute | solution.py:68
  365.4 20.0 %collective-permute-done = f32[2,4,1,128,128]{4,3,2,1,0:T(8,128)} collective-permute-done((f32[2,4,1,128,128]{4,3,2,1,0:T(8,128)S(1)}, f32[2,4,1,128,128]{4,3,2,1,0:T(8,128)}, u32[]{:S(2)}, u32[]{:S(2)}) %collective-permute-start) | collective-permute-done | bytes 524320 | tf_op jit(solution)/shard_map/while/body/eval_jaxpr/ppermute | solution.py:68
  395.4 23.6 %all-to-all-start.4 = ((f32[8,2,2,4,2,8,128]{6,5,4,3,2,1,0:T(8,128)}), f32[8,2,2,4,2,8,128]{6,5,4,3,2,1,0:T(8,128)S(1)}, u32[]{:S(2)}, u32[]{:S(2)}) async-start(f32[8,2,2,4,2,8,128]{6,5,4,3,2,1,0:T(8,128)} %copy.90), calls=%async_computation.4 | async-start | bytes 2097152 | tf_op jit(solution)/shard_map/all_to_all | solution.py:50
  419.4 15.6 %all-to-all-done.4 = f32[8,2,2,4,2,8,128]{6,5,4,3,2,1,0:T(8,128)S(1)} async-done(((f32[8,2,2,4,2,8,128]{6,5,4,3,2,1,0:T(8,128)}), f32[8,2,2,4,2,8,128]{6,5,4,3,2,1,0:T(8,128)S(1)}, u32[]{:S(2)}, u32[]{:S(2)}) %all-to-all-start.4) | async-done | bytes 1048608 | tf_op jit(solution)/shard_map/all_to_all | solution.py:50
  437.0 13.7 %all_to_all.58 = f32[32,4,8,128]{3,2,1,0:T(8,128)S(1)} all-to-all(f32[32,4,8,128]{3,2,1,0:T(8,128)S(1)} %copy.96), channel_id=1, replica_groups=mesh['tm_0'=4,'tm_1'=2,'tm_2'=2,'space'=16] {'tm_0','tm_1','tm_2'}, dimensions={0} | all-to-all | bytes 1048576 | tf_op jit(solution)/shard_map/all_to_all | solution.py:27
  (135 shorter events, 145.9 us)
Async XLA Ops:
  4.0 16.6 %all-to-all-start = ((f32[2,4,128,128]{3,1,0,2:T(4,128)}), f32[2,4,128,128]{3,1,0,2:T(4,128)S(1)}, u32[]{:S(2)}, u32[]{:S(2)}) async-start(f32[2,4,128,128]{3,1,0,2:T(4,128)} %pad_maximum_fusion.5), calls=%async_computation | async-start | bytes 1048576 | tf_op jit(solution)/shard_map/all_to_all | solution.py:27
  29.1 20.0 %all-to-all-start.2 = ((f32[8,2,2,4,2,8,128]{6,2,1,5,4,3,0:T(2,128)}), f32[8,2,2,4,2,8,128]{6,2,1,5,4,3,0:T(2,128)S(1)}, u32[]{:S(2)}, u32[]{:S(2)}) async-start(f32[8,2,2,4,2,8,128]{6,2,1,5,4,3,0:T(2,128)} %copy.85), calls=%async_computation.2 | async-start | bytes 2097152 | tf_op jit(solution)/shard_map/all_to_all | solution.py:50
  50.1 26.3 %collective-permute-start = (f32[2,4,1,128,128]{4,3,2,1,0:T(8,128)S(1)}, f32[2,4,1,128,128]{4,3,2,1,0:T(8,128)}, u32[]{:S(2)}, u32[]{:S(2)}) collective-permute-start(f32[2,4,1,128,128]{4,3,2,1,0:T(8,128)S(1)} %get-tuple-element.276), channel_id=1, source_target_pairs={{0,1},{1,2},{2,3},{3,4},{4,5},{5,6},{6,7},{7,8},{8,9},{9,10},{10,1... | collective-permute-start | bytes 1572872 | tf_op jit(solution)/shard_map/while/body/eval_jaxpr/ppermute | solution.py:68
  55.3 30.2 %collective-permute-start.1 = (f32[2,4,1,128,128]{4,3,2,1,0:T(8,128)S(1)}, f32[2,4,1,128,128]{4,3,2,1,0:T(8,128)}, u32[]{:S(2)}, u32[]{:S(2)}) collective-permute-start(f32[2,4,1,128,128]{4,3,2,1,0:T(8,128)S(1)} %get-tuple-element.277), channel_id=1, source_target_pairs={{1,0},{2,1},{3,2},{4,3},{5,4},{6,5},{7,6},{8,7},{9,8},{10,9},{11,1... | collective-permute-start | bytes 1572872 | tf_op jit(solution)/shard_map/while/body/eval_jaxpr/ppermute | solution.py:70
  88.1 21.5 %collective-permute-start = (f32[2,4,1,128,128]{4,3,2,1,0:T(8,128)S(1)}, f32[2,4,1,128,128]{4,3,2,1,0:T(8,128)}, u32[]{:S(2)}, u32[]{:S(2)}) collective-permute-start(f32[2,4,1,128,128]{4,3,2,1,0:T(8,128)S(1)} %get-tuple-element.276), channel_id=1, source_target_pairs={{0,1},{1,2},{2,3},{3,4},{4,5},{5,6},{6,7},{7,8},{8,9},{9,10},{10,1... | collective-permute-start | bytes 1572872 | tf_op jit(solution)/shard_map/while/body/eval_jaxpr/ppermute | solution.py:68
  90.1 27.7 %collective-permute-start.1 = (f32[2,4,1,128,128]{4,3,2,1,0:T(8,128)S(1)}, f32[2,4,1,128,128]{4,3,2,1,0:T(8,128)}, u32[]{:S(2)}, u32[]{:S(2)}) collective-permute-start(f32[2,4,1,128,128]{4,3,2,1,0:T(8,128)S(1)} %get-tuple-element.277), channel_id=1, source_target_pairs={{1,0},{2,1},{3,2},{4,3},{5,4},{6,5},{7,6},{8,7},{9,8},{10,9},{11,1... | collective-permute-start | bytes 1572872 | tf_op jit(solution)/shard_map/while/body/eval_jaxpr/ppermute | solution.py:70
  120.5 20.4 %collective-permute-start = (f32[2,4,1,128,128]{4,3,2,1,0:T(8,128)S(1)}, f32[2,4,1,128,128]{4,3,2,1,0:T(8,128)}, u32[]{:S(2)}, u32[]{:S(2)}) collective-permute-start(f32[2,4,1,128,128]{4,3,2,1,0:T(8,128)S(1)} %get-tuple-element.276), channel_id=1, source_target_pairs={{0,1},{1,2},{2,3},{3,4},{4,5},{5,6},{6,7},{7,8},{8,9},{9,10},{10,1... | collective-permute-start | bytes 1572872 | tf_op jit(solution)/shard_map/while/body/eval_jaxpr/ppermute | solution.py:68
  122.4 23.3 %collective-permute-start.1 = (f32[2,4,1,128,128]{4,3,2,1,0:T(8,128)S(1)}, f32[2,4,1,128,128]{4,3,2,1,0:T(8,128)}, u32[]{:S(2)}, u32[]{:S(2)}) collective-permute-start(f32[2,4,1,128,128]{4,3,2,1,0:T(8,128)S(1)} %get-tuple-element.277), channel_id=1, source_target_pairs={{1,0},{2,1},{3,2},{4,3},{5,4},{6,5},{7,6},{8,7},{9,8},{10,9},{11,1... | collective-permute-start | bytes 1572872 | tf_op jit(solution)/shard_map/while/body/eval_jaxpr/ppermute | solution.py:70
  148.4 15.0 %collective-permute-start = (f32[2,4,1,128,128]{4,3,2,1,0:T(8,128)S(1)}, f32[2,4,1,128,128]{4,3,2,1,0:T(8,128)}, u32[]{:S(2)}, u32[]{:S(2)}) collective-permute-start(f32[2,4,1,128,128]{4,3,2,1,0:T(8,128)S(1)} %get-tuple-element.276), channel_id=1, source_target_pairs={{0,1},{1,2},{2,3},{3,4},{4,5},{5,6},{6,7},{7,8},{8,9},{9,10},{10,1... | collective-permute-start | bytes 1572872 | tf_op jit(solution)/shard_map/while/body/eval_jaxpr/ppermute | solution.py:68
  152.4 19.3 %collective-permute-start.1 = (f32[2,4,1,128,128]{4,3,2,1,0:T(8,128)S(1)}, f32[2,4,1,128,128]{4,3,2,1,0:T(8,128)}, u32[]{:S(2)}, u32[]{:S(2)}) collective-permute-start(f32[2,4,1,128,128]{4,3,2,1,0:T(8,128)S(1)} %get-tuple-element.277), channel_id=1, source_target_pairs={{1,0},{2,1},{3,2},{4,3},{5,4},{6,5},{7,6},{8,7},{9,8},{10,9},{11,1... | collective-permute-start | bytes 1572872 | tf_op jit(solution)/shard_map/while/body/eval_jaxpr/ppermute | solution.py:70
  176.3 23.5 %collective-permute-start.1 = (f32[2,4,1,128,128]{4,3,2,1,0:T(8,128)S(1)}, f32[2,4,1,128,128]{4,3,2,1,0:T(8,128)}, u32[]{:S(2)}, u32[]{:S(2)}) collective-permute-start(f32[2,4,1,128,128]{4,3,2,1,0:T(8,128)S(1)} %get-tuple-element.277), channel_id=1, source_target_pairs={{1,0},{2,1},{3,2},{4,3},{5,4},{6,5},{7,6},{8,7},{9,8},{10,9},{11,1... | collective-permute-start | bytes 1572872 | tf_op jit(solution)/shard_map/while/body/eval_jaxpr/ppermute | solution.py:70
  202.6 15.8 %collective-permute-start = (f32[2,4,1,128,128]{4,3,2,1,0:T(8,128)S(1)}, f32[2,4,1,128,128]{4,3,2,1,0:T(8,128)}, u32[]{:S(2)}, u32[]{:S(2)}) collective-permute-start(f32[2,4,1,128,128]{4,3,2,1,0:T(8,128)S(1)} %get-tuple-element.276), channel_id=1, source_target_pairs={{0,1},{1,2},{2,3},{3,4},{4,5},{5,6},{6,7},{7,8},{8,9},{9,10},{10,1... | collective-permute-start | bytes 1572872 | tf_op jit(solution)/shard_map/while/body/eval_jaxpr/ppermute | solution.py:68
  204.5 24.9 %collective-permute-start.1 = (f32[2,4,1,128,128]{4,3,2,1,0:T(8,128)S(1)}, f32[2,4,1,128,128]{4,3,2,1,0:T(8,128)}, u32[]{:S(2)}, u32[]{:S(2)}) collective-permute-start(f32[2,4,1,128,128]{4,3,2,1,0:T(8,128)S(1)} %get-tuple-element.277), channel_id=1, source_target_pairs={{1,0},{2,1},{3,2},{4,3},{5,4},{6,5},{7,6},{8,7},{9,8},{10,9},{11,1... | collective-permute-start | bytes 1572872 | tf_op jit(solution)/shard_map/while/body/eval_jaxpr/ppermute | solution.py:70
  232.2 15.8 %collective-permute-start = (f32[2,4,1,128,128]{4,3,2,1,0:T(8,128)S(1)}, f32[2,4,1,128,128]{4,3,2,1,0:T(8,128)}, u32[]{:S(2)}, u32[]{:S(2)}) collective-permute-start(f32[2,4,1,128,128]{4,3,2,1,0:T(8,128)S(1)} %get-tuple-element.276), channel_id=1, source_target_pairs={{0,1},{1,2},{2,3},{3,4},{4,5},{5,6},{6,7},{7,8},{8,9},{9,10},{10,1... | collective-permute-start | bytes 1572872 | tf_op jit(solution)/shard_map/while/body/eval_jaxpr/ppermute | solution.py:68
  234.1 24.2 %collective-permute-start.1 = (f32[2,4,1,128,128]{4,3,2,1,0:T(8,128)S(1)}, f32[2,4,1,128,128]{4,3,2,1,0:T(8,128)}, u32[]{:S(2)}, u32[]{:S(2)}) collective-permute-start(f32[2,4,1,128,128]{4,3,2,1,0:T(8,128)S(1)} %get-tuple-element.277), channel_id=1, source_target_pairs={{1,0},{2,1},{3,2},{4,3},{5,4},{6,5},{7,6},{8,7},{9,8},{10,9},{11,1... | collective-permute-start | bytes 1572872 | tf_op jit(solution)/shard_map/while/body/eval_jaxpr/ppermute | solution.py:70
  261.0 25.4 %collective-permute-start = (f32[2,4,1,128,128]{4,3,2,1,0:T(8,128)S(1)}, f32[2,4,1,128,128]{4,3,2,1,0:T(8,128)}, u32[]{:S(2)}, u32[]{:S(2)}) collective-permute-start(f32[2,4,1,128,128]{4,3,2,1,0:T(8,128)S(1)} %get-tuple-element.276), channel_id=1, source_target_pairs={{0,1},{1,2},{2,3},{3,4},{4,5},{5,6},{6,7},{7,8},{8,9},{9,10},{10,1... | collective-permute-start | bytes 1572872 | tf_op jit(solution)/shard_map/while/body/eval_jaxpr/ppermute | solution.py:68
  268.4 22.7 %collective-permute-start.1 = (f32[2,4,1,128,128]{4,3,2,1,0:T(8,128)S(1)}, f32[2,4,1,128,128]{4,3,2,1,0:T(8,128)}, u32[]{:S(2)}, u32[]{:S(2)}) collective-permute-start(f32[2,4,1,128,128]{4,3,2,1,0:T(8,128)S(1)} %get-tuple-element.277), channel_id=1, source_target_pairs={{1,0},{2,1},{3,2},{4,3},{5,4},{6,5},{7,6},{8,7},{9,8},{10,9},{11,1... | collective-permute-start | bytes 1572872 | tf_op jit(solution)/shard_map/while/body/eval_jaxpr/ppermute | solution.py:70
  293.8 22.6 %collective-permute-start = (f32[2,4,1,128,128]{4,3,2,1,0:T(8,128)S(1)}, f32[2,4,1,128,128]{4,3,2,1,0:T(8,128)}, u32[]{:S(2)}, u32[]{:S(2)}) collective-permute-start(f32[2,4,1,128,128]{4,3,2,1,0:T(8,128)S(1)} %get-tuple-element.276), channel_id=1, source_target_pairs={{0,1},{1,2},{2,3},{3,4},{4,5},{5,6},{6,7},{7,8},{8,9},{9,10},{10,1... | collective-permute-start | bytes 1572872 | tf_op jit(solution)/shard_map/while/body/eval_jaxpr/ppermute | solution.py:68
  297.9 26.6 %collective-permute-start.1 = (f32[2,4,1,128,128]{4,3,2,1,0:T(8,128)S(1)}, f32[2,4,1,128,128]{4,3,2,1,0:T(8,128)}, u32[]{:S(2)}, u32[]{:S(2)}) collective-permute-start(f32[2,4,1,128,128]{4,3,2,1,0:T(8,128)S(1)} %get-tuple-element.277), channel_id=1, source_target_pairs={{1,0},{2,1},{3,2},{4,3},{5,4},{6,5},{7,6},{8,7},{9,8},{10,9},{11,1... | collective-permute-start | bytes 1572872 | tf_op jit(solution)/shard_map/while/body/eval_jaxpr/ppermute | solution.py:70
  327.2 24.8 %collective-permute-start = (f32[2,4,1,128,128]{4,3,2,1,0:T(8,128)S(1)}, f32[2,4,1,128,128]{4,3,2,1,0:T(8,128)}, u32[]{:S(2)}, u32[]{:S(2)}) collective-permute-start(f32[2,4,1,128,128]{4,3,2,1,0:T(8,128)S(1)} %get-tuple-element.276), channel_id=1, source_target_pairs={{0,1},{1,2},{2,3},{3,4},{4,5},{5,6},{6,7},{7,8},{8,9},{9,10},{10,1... | collective-permute-start | bytes 1572872 | tf_op jit(solution)/shard_map/while/body/eval_jaxpr/ppermute | solution.py:68
  329.1 26.7 %collective-permute-start.1 = (f32[2,4,1,128,128]{4,3,2,1,0:T(8,128)S(1)}, f32[2,4,1,128,128]{4,3,2,1,0:T(8,128)}, u32[]{:S(2)}, u32[]{:S(2)}) collective-permute-start(f32[2,4,1,128,128]{4,3,2,1,0:T(8,128)S(1)} %get-tuple-element.277), channel_id=1, source_target_pairs={{1,0},{2,1},{3,2},{4,3},{5,4},{6,5},{7,6},{8,7},{9,8},{10,9},{11,1... | collective-permute-start | bytes 1572872 | tf_op jit(solution)/shard_map/while/body/eval_jaxpr/ppermute | solution.py:70
  358.5 26.8 %collective-permute-start = (f32[2,4,1,128,128]{4,3,2,1,0:T(8,128)S(1)}, f32[2,4,1,128,128]{4,3,2,1,0:T(8,128)}, u32[]{:S(2)}, u32[]{:S(2)}) collective-permute-start(f32[2,4,1,128,128]{4,3,2,1,0:T(8,128)S(1)} %get-tuple-element.276), channel_id=1, source_target_pairs={{0,1},{1,2},{2,3},{3,4},{4,5},{5,6},{6,7},{7,8},{8,9},{9,10},{10,1... | collective-permute-start | bytes 1572872 | tf_op jit(solution)/shard_map/while/body/eval_jaxpr/ppermute | solution.py:68
  363.5 23.5 %collective-permute-start.1 = (f32[2,4,1,128,128]{4,3,2,1,0:T(8,128)S(1)}, f32[2,4,1,128,128]{4,3,2,1,0:T(8,128)}, u32[]{:S(2)}, u32[]{:S(2)}) collective-permute-start(f32[2,4,1,128,128]{4,3,2,1,0:T(8,128)S(1)} %get-tuple-element.277), channel_id=1, source_target_pairs={{1,0},{2,1},{3,2},{4,3},{5,4},{6,5},{7,6},{8,7},{9,8},{10,9},{11,1... | collective-permute-start | bytes 1572872 | tf_op jit(solution)/shard_map/while/body/eval_jaxpr/ppermute | solution.py:70
  395.4 39.6 %all-to-all-start.4 = ((f32[8,2,2,4,2,8,128]{6,5,4,3,2,1,0:T(8,128)}), f32[8,2,2,4,2,8,128]{6,5,4,3,2,1,0:T(8,128)S(1)}, u32[]{:S(2)}, u32[]{:S(2)}) async-start(f32[8,2,2,4,2,8,128]{6,5,4,3,2,1,0:T(8,128)} %copy.90), calls=%async_computation.4 | async-start | bytes 2097152 | tf_op jit(solution)/shard_map/all_to_all | solution.py:50
  (2 other events, 18.1 us)
where the time goes:
time: 453 us; the launch traced here: 452 us
  waiting for transfers between devices  282 us (62%)
  starting transfers between devices  103 us (23%)
  other arithmetic  30.8 us (7%)
  blocking collectives  22.8 us (5%)
  local copies, waits for them, and re-layouts  8.98 us (2%)
    ppermute x11, waiting for transfers between devices, padded_2(): lax.ppermute(tail, axis, [(i, (i + 1) % count) for i in range(ends)])  158 us
    ppermute x11, waiting for transfers between devices, padded_2(): lax.ppermute(head, axis, [((i + 1) % count, i) for i in range(ends)])  81.2 us
    ppermute x11, starting transfers between devices, padded_2(): lax.ppermute(tail, axis, [(i, (i + 1) % count) for i in range(ends)])  37.1 us
    ppermute x11, starting transfers between devices, padded_2(): lax.ppermute(head, axis, [((i + 1) % count, i) for i in range(ends)])  33.1 us
    all_to_all x2, waiting for transfers between devices, moved_by_axis(): lax.all_to_all(pieces, axes[k], split_axis=k, concat_axis=k, tiled=True)  31.7 us
    all_to_all x2, starting transfers between devices, moved_by_axis(): lax.all_to_all(pieces, axes[k], split_axis=k, concat_axis=k, tiled=True)  27.2 us
    add x11, other arithmetic, sweep(): return block_solve(coefficient, sources + MU * neighbour_sum(zpadded))  19.8 us
    all_to_all x1, blocking collectives, in_one_piece(): lax.all_to_all(both, axis, split_axis=split_dim, concat_axis=concat_dim,...  13.7 us
  transfers between devices with their start and end apart: 25, of which 25 were waited for; matrix products, arithmetic and copies ran while one was open for 0% of the time, Pallas kernels for 0%

commit v1 on v0

v1 whole, which is shorter than its diff:
```python
import math

import jax
import jax.numpy as jnp
from jax import lax
from jax.experimental import pallas as pl
from jax.experimental.pallas import tpu as pltpu
from jax.sharding import PartitionSpec as P

STEPS = 32
SWEEPS = 12
ALPHA = 0.1
MESH = pl.DeviceIdType.MESH
HALO = 8
TAIL = 3
ROWS = 16 + 2 * HALO
F32 = jnp.float32


def device(x, z, core, y):
    return (x * 4 + (z % 2) * 2 + core, (z // 2) * 4 + y)


def mul_const(v, c):
    re, im = v
    cr, ci = c.real, c.imag
    if abs(ci) < 1e-12:
        if abs(cr - 1.0) < 1e-12:
            return v
        return (re * cr, im * cr)
    if abs(cr) < 1e-12:
        if abs(ci - 1.0) < 1e-12:
            return (-im, re)
        if abs(ci + 1.0) < 1e-12:
            return (im, -re)
        return (im * (-ci), re * ci)
    return (re * cr - im * ci, re * ci + im * cr)


def add(a, b):
    return (a[0] + b[0], a[1] + b[1])


def sub(a, b):
    return (a[0] - b[0], a[1] - b[1])


def small_dft(values, sign):
    n = len(values)
    if n == 1:
        return values
    even = small_dft(values[0::2], sign)
    odd = small_dft(values[1::2], sign)
    out = [None] * n
    for k in range(n // 2):
        angle = sign * 2.0 * math.pi * k / n
        t = mul_const(odd[k], complex(math.cos(angle), math.sin(angle)))
        out[k] = add(even[k], t)
        out[k + n // 2] = sub(even[k], t)
    return out


def long_dft(load, store, tmp, sign):
    for b in range(8):
        group = small_dft([load(8 * a + b) for a in range(4)], sign)
        for k1 in range(4):
            angle = sign * 2.0 * math.pi * b * k1 / 32
            re, im = mul_const(group[k1], complex(math.cos(angle), math.sin(angle)))
            tmp[8 * k1 + b, 0] = re
            tmp[8 * k1 + b, 1] = im
    for k1 in range(4):
        group = small_dft([(tmp[8 * k1 + b, 0], tmp[8 * k1 + b, 1]) for b in range(8)], sign)
        for k2 in range(8):
            store(k1 + 4 * k2, group[k2])


def kernel(
    state, adjoint, reaction, out,
    src, rsrc, r1, rf, rh, b1, tmp, f1, fld, fh, s, w, u0, u1, hal, g, f2, b2,
    load_sem, send_sem, recv_sem,
):
    tm = lax.axis_index("tm")
    sp = lax.axis_index("space")
    x, zlo, core = tm // 4, (tm // 2) % 2, tm % 2
    zhi, y = sp // 4, sp % 4
    z = zhi * 2 + zlo
    zhh, par = zhi // 2, zhi % 2
    zp, rtl = x // 2, x % 2
    freq = x * 8 + y * 2 + core
    zlow = core * 8 + y * 2 + zp
    up, down = (z + 1) % 8, (z + 7) % 8
    home = core == par

    loads = [
        pltpu.make_async_copy(reaction, rsrc, load_sem.at[2]),
        pltpu.make_async_copy(state, src.at[0], load_sem.at[0]),
        pltpu.make_async_copy(adjoint, src.at[1], load_sem.at[1]),
    ]
    for c in loads:
        c.start()

    barrier = pltpu.get_barrier_semaphore()

    def greet(dev):
        pl.semaphore_signal(barrier, inc=1, device_id=dev, device_id_type=MESH)

    def greet_plane(i, _):
        xx, zz = (x + i // 8) % 4, (z + i) % 8
        here = jnp.logical_and(home, i == 0)

        @pl.when(jnp.logical_not(here))
        def _():
            greet(device(xx, zz, par, y))

        return 0

    lax.fori_loop(0, 32, greet_plane, 0)

    def source_of(i):
        xx, cc, ll = (x + i // 8) % 4, (core + (i // 4) % 2) % 2, (zlo + (i // 2) % 2) % 2
        hh = (zhh + i % 2) % 2
        return xx, (core + 2 * hh) * 2 + ll, cc, hh

    def greet_source(i, _):
        xx, zz, cc, hh = source_of(i)
        here = jnp.logical_and(home, i == 0)

        @pl.when(jnp.logical_not(here))
        def _():
            greet(device(xx, zz, cc, y))

        return 0

    lax.fori_loop(0, 32, greet_source, 0)

    def mate(i):
        return (x + i // 8) % 4, (y + (i // 2) % 4) % 4, (core + i % 2) % 2

    def greet_mate(i, _):
        xx, yy, cc = mate(i)
        greet(device(xx, z, cc, yy))
        return 0

    lax.fori_loop(1, 32, greet_mate, 0)
    greet(device(x, up, core, y))
    greet(device(x, down, core, y))
    pl.semaphore_wait(barrier, 97 - 2 * home.astype(jnp.int32))

    def copy_to(src_ref, dst_ref, phase, dev):
        return pltpu.make_async_remote_copy(
            src_ref=src_ref, dst_ref=dst_ref, send_sem=send_sem.at[phase],
            recv_sem=recv_sem.at[phase], device_id=dev, device_id_type=MESH,
        )

    def copy_here(src_ref, dst_ref, phase):
        return pltpu.make_async_copy(src_ref, dst_ref, recv_sem.at[phase])

    def arrived(ref, phase):
        pltpu.make_async_copy(ref, ref, recv_sem.at[phase]).wait()

    def sent(ref, phase):
        pltpu.make_async_copy(ref, ref, send_sem.at[phase]).wait()

    loads[0].wait()
    for i in range(2):
        zz = zlo * 4 + core * 2 + i
        tile = rsrc.at[zp, 2 * zz + rtl]
        here = jnp.logical_and(home, zz == z)

        @pl.when(here)
        def _():
            copy_here(tile, r1.at[zhh], 0).start()

        @pl.when(jnp.logical_not(here))
        def _():
            copy_to(tile, r1.at[zhh], 0, device(x, zz, par, y)).start()

    loads[1].wait()
    loads[2].wait()

    def first(i, _):
        xx, zz = (x + i // 8) % 4, (z + i) % 8
        piece = src.at[:, :, xx // 2, 2 * zz + xx % 2]
        place = b1.at[zhh, :, pl.ds(2 * tm, 2)]
        here = jnp.logical_and(home, i == 0)

        @pl.when(here)
        def _():
            copy_here(piece, place, 1).start()

        @pl.when(jnp.logical_not(here))
        def _():
            copy_to(piece, place, 1, device(xx, zz, par, y)).start()

        return 0

    lax.fori_loop(0, 32, first, 0)

    arrived(r1, 0)
    copy_here(r1, rf.at[:, zlow, rtl], 2).start()

    def spread_reaction(i, _):
        xx, yy, cc = mate(i)
        copy_to(r1, rf.at[:, zlow, rtl], 2, device(xx, z, cc, yy)).start()
        return 0

    lax.fori_loop(1, 32, spread_reaction, 0)
    arrived(rf, 2)
    copy_to(rf.at[:, :, 0], rh.at[1], 3, device(x, down, core, y)).start()
    copy_to(rf.at[:, :, 1], rh.at[0], 4, device(x, up, core, y)).start()

    cos_k, sin_k = jnp.float32(0.0), jnp.float32(0.0)
    for k in range(STEPS):
        angle = 2.0 * math.pi * k / STEPS
        cos_k = jnp.where(freq == k, jnp.float32(math.cos(angle)), cos_k)
        sin_k = jnp.where(freq == k, jnp.float32(math.sin(angle)), sin_k)
    rate = math.exp(math.log(ALPHA) / STEPS)
    base_re = 1.0 - rate * cos_k + 6.0
    d_im = rate * sin_k + 1.0

    def coefficient(row, j, value, keep):
        d_re = base_re + value
        inv = 1.0 / (d_re * d_re + d_im * d_im)
        w_re = d_re * inv
        w_im = -d_im * inv
        if keep is not None:
            w_re = jnp.where(keep, w_re, 0.0)
            w_im = jnp.where(keep, w_im, 0.0)
        w[row, 0, j] = w_re
        w[row, 1, j] = w_im

    rfl = rf.reshape(512, 128)
    rhl = rh.reshape(512, 128)

    def inner_rows(r, _):
        for t in range(2):
            for j in range(4):
                value = rfl[pl.ds(j * 16 + t * 8 + r, 8, stride=64), :]
                coefficient(HALO + t * 8 + r, j, value, None)
        return 0

    lax.fori_loop(0, 8, inner_rows, 0)

    arrived(b1, 1)
    for tile in range(2):

        def load(n):
            growth = math.exp(math.log(ALPHA) * n / STEPS)
            return (b1[tile, 0, n] * growth, b1[tile, 1, STEPS - 1 - n] * growth)

        def store(k, v):
            f1[k, tile, 0] = v[0]
            f1[k, tile, 1] = v[1]

        long_dft(load, store, tmp, -1)

    def second(i, _):
        xx, yy, cc = mate(i)
        copy_to(f1.at[xx * 8 + yy * 2 + cc], fld.at[:, zlow, rtl], 5, device(xx, z, cc, yy)).start()
        return 0

    copy_here(f1.at[freq], fld.at[:, zlow, rtl], 5).start()
    lax.fori_loop(1, 32, second, 0)

    arrived(rh.at[1], 3)
    arrived(rh.at[0], 4)

    def outer_rows(r, _):
        for side in range(2):
            keep = (z > 0) if side == 0 else (z < 7)
            for j in range(4):
                value = rhl[pl.ds(side * 256 + j * 8 + r, 8, stride=32), :]
                coefficient(side * (HALO + 16) + r, j, value, keep)
        return 0

    lax.fori_loop(0, 8, outer_rows, 0)

    arrived(fld, 5)
    copy_to(fld.at[:, :, 0], fh.at[1], 6, device(x, down, core, y)).start()
    copy_to(fld.at[:, :, 1], fh.at[0], 7, device(x, up, core, y)).start()

    fll = fld.reshape(1024, 128)
    fhl = fh.reshape(1024, 128)

    def start_row(row, j, v):
        s[row, 0, j] = v[0]
        s[row, 1, j] = v[1]
        w_re, w_im = w[row, 0, j], w[row, 1, j]
        u0[row, 0, j] = w_re * v[0] - w_im * v[1]
        u0[row, 1, j] = w_re * v[1] + w_im * v[0]

    def inner_start(r, _):
        for t in range(2):
            for j in range(4):
                v = [fll[pl.ds(j * 32 + t * 16 + c * 8 + r, 8, stride=128), :] for c in range(2)]
                start_row(HALO + t * 8 + r, j, v)
        return 0

    lax.fori_loop(0, 8, inner_start, 0)
    arrived(fh.at[1], 6)
    arrived(fh.at[0], 7)

    def outer_start(r, _):
        for side in range(2):
            for j in range(4):
                v = [fhl[pl.ds(side * 512 + j * 16 + c * 8 + r, 8, stride=64), :] for c in range(2)]
                start_row(side * (HALO + 16) + r, j, v)
        return 0

    lax.fori_loop(0, 8, outer_start, 0)

    lanes = lax.broadcasted_iota(jnp.int32, (8, 128), 1)
    subs = lax.broadcasted_iota(jnp.int32, (8, 128), 0)
    first_lane, last_lane = lanes == 0, lanes == 127
    first_sub, last_sub = subs == 0, subs == 7

    def sweep_row(old, new, row):
        total = [[None] * 4, [None] * 4]
        for c in range(2):
            mid = [old[row, c, j] for j in range(4)]
            before = jnp.where(first_sub, 0.0, pltpu.roll(mid[3], 1, 0))
            after = jnp.where(last_sub, 0.0, pltpu.roll(mid[0], 7, 0))
            line = [before] + mid + [after]
            for j in range(4):
                t = s[row, c, j] + (line[j] + line[j + 2])
                t = t + (old[row - 1, c, j] + old[row + 1, c, j])
                left = jnp.where(first_lane, 0.0, pltpu.roll(mid[j], 1, 1))
                right = jnp.where(last_lane, 0.0, pltpu.roll(mid[j], 127, 1))
                total[c][j] = t + (left + right)
        for j in range(4):
            w_re, w_im = w[row, 0, j], w[row, 1, j]
            t_re, t_im = total[0][j], total[1][j]
            new[row, 0, j] = w_re * t_re - w_im * t_im
            new[row, 1, j] = w_re * t_im + w_im * t_re

    def sweep(old, new, low, high):
        count = high - low

        def four(i, _):
            for k in range(4):
                sweep_row(old, new, low + 4 * i + k)
            return 0

        lax.fori_loop(0, count // 4, four, 0)
        for row in range(low + count // 4 * 4, high):
            sweep_row(old, new, row)

    pair = [u0, u1]
    for m in range(1, HALO + 1):
        sweep(pair[(m + 1) % 2], pair[m % 2], m, ROWS - m)
    last = pair[HALO % 2]
    copy_to(last.at[pl.ds(HALO, TAIL)], hal.at[1], 8, device(x, down, core, y)).start()
    copy_to(last.at[pl.ds(HALO + 16 - TAIL, TAIL)], hal.at[0], 9, device(x, up, core, y)).start()
    arrived(hal.at[1], 8)
    arrived(hal.at[0], 9)
    for k in range(TAIL):
        for c in range(2):
            for j in range(4):
                last[HALO - TAIL + k, c, j] = jnp.where(z > 0, hal[0, k, c, j], 0.0)
                last[HALO + 16 + k, c, j] = jnp.where(z < 7, hal[1, k, c, j], 0.0)
    for m in range(HALO + 1, SWEEPS):
        margin = SWEEPS - 1 - m
        if m == HALO + 2:
            sent(hal.at[1], 8)
            sent(hal.at[0], 9)
        sweep(pair[(m + 1) % 2], pair[m % 2], HALO - margin, HALO + 16 + margin)
    result = pair[(SWEEPS - 1) % 2]

    gl = g.reshape(1024, 128)

    def turn_back(r, _):
        for t in range(2):
            for j in range(4):
                for c in range(2):
                    gl[pl.ds(j * 32 + t * 16 + c * 8 + r, 8, stride=128), :] = result[HALO + t * 8 + r, c, j]
        return 0

    lax.fori_loop(0, 8, turn_back, 0)

    def third(i, _):
        xx, yy, cc = mate(i)
        piece = g.at[:, cc * 8 + yy * 2 + xx // 2, xx % 2]
        copy_to(piece, f2.at[freq], 10, device(xx, z, cc, yy)).start()
        return 0

    copy_here(g.at[:, zlow, rtl], f2.at[freq], 10).start()
    lax.fori_loop(1, 32, third, 0)
    arrived(f2, 10)

    for tile in range(2):

        def load(k):
            return (f2[k, tile, 0], f2[k, tile, 1])

        def store(n, v):
            shrink = math.exp(-math.log(ALPHA) * n / STEPS) / STEPS
            b2[tile, 0, n] = v[0] * shrink
            b2[tile, 1, STEPS - 1 - n] = v[1] * shrink

        long_dft(load, store, tmp, 1)

    def fourth(i, _):
        xx, zz, cc, hh = source_of(i)
        times = pl.ds(2 * (xx * 4 + (zz % 2) * 2 + cc), 2)
        piece = b2.at[hh, :, times]
        place = out.at[:, :, zp, 2 * z + rtl]
        here = jnp.logical_and(home, i == 0)

        @pl.when(here)
        def _():
            copy_here(piece, place, 11).start()

        @pl.when(jnp.logical_not(here))
        def _():
            copy_to(piece, place, 11, device(xx, zz, cc, y)).start()

        return 0

    lax.fori_loop(0, 32, fourth, 0)

    for i in range(2):
        zz = zlo * 4 + core * 2 + i

        @pl.when(jnp.logical_not(jnp.logical_and(home, zz == z)))
        def _():
            sent(r1.at[0], 0)

    sent(rh.at[1], 3)
    sent(rh.at[0], 4)
    sent(fh.at[1], 6)
    sent(fh.at[0], 7)

    def drain(i, _):
        sent(r1, 2)
        sent(f1.at[0], 5)
        sent(f2.at[0], 10)
        sent(f1.at[0], 1)
        sent(f1.at[0], 11)
        return 0

    lax.fori_loop(1, 32, drain, 0)

    @pl.when(jnp.logical_not(home))
    def _():
        sent(f1.at[0], 1)
        sent(f1.at[0], 11)

    arrived(out, 11)


def body(state_rhs, adjoint_rhs, reaction):
    tile = (8, 128)
    field = pltpu.VMEM((ROWS, 2, 4) + tile, F32)
    result = pl.pallas_call(
        kernel,
        out_shape=jax.ShapeDtypeStruct((2, 2, 2, 16) + tile, F32),
        in_specs=[pl.BlockSpec(memory_space=pl.ANY)] * 3,
        out_specs=pl.BlockSpec(memory_space=pl.ANY),
        scratch_shapes=[
            pltpu.VMEM((2, 2, 2, 16) + tile, F32),
            pltpu.VMEM((2, 16) + tile, F32),
            pltpu.VMEM((2,) + tile, F32),
            pltpu.VMEM((2, 16, 2) + tile, F32),
            pltpu.VMEM((2, 2, 16) + tile, F32),
            pltpu.VMEM((2, 2, 32) + tile, F32),
            pltpu.VMEM((32, 2) + tile, F32),
            pltpu.VMEM((32, 2, 2) + tile, F32),
            pltpu.VMEM((2, 16, 2, 2) + tile, F32),
            pltpu.VMEM((2, 2, 16, 2) + tile, F32),
            field,
            field,
            field,
            field,
            pltpu.VMEM((2, TAIL, 2, 4) + tile, F32),
            pltpu.VMEM((2, 16, 2, 2) + tile, F32),
            pltpu.VMEM((32, 2, 2) + tile, F32),
            pltpu.VMEM((2, 2, 32) + tile, F32),
            pltpu.SemaphoreType.DMA((3,)),
            pltpu.SemaphoreType.DMA((12,)),
            pltpu.SemaphoreType.DMA((12,)),
        ],
        compiler_params=pltpu.CompilerParams(collective_id=0, has_side_effects=True),
        name="precondition",
    )(
        state_rhs.reshape((2, 2, 16) + tile),
        adjoint_rhs.reshape((2, 2, 16) + tile),
        reaction.reshape((2, 16) + tile),
    )
    return (result[0].reshape(state_rhs.shape), result[1].reshape(state_rhs.shape))


def solution(mesh):
    placed = P("tm", "space", None, None)
    return jax.shard_map(
        body,
        mesh=mesh,
        in_specs=(placed, placed, P("space", None, None)),
        out_specs=(placed, placed),
        check_vma=False,
    )
```

time: 453 us -> 85.5 us (0.19)
  the two profiles are of different devices: /device:TPU:88 before, /device:TPU:1 now
where the time goes in v1:
time: 85.5 us; the launch traced here: 85.4 us
  Pallas kernels  82.9 us (97%)
  local copies, waits for them, and re-layouts  1.86 us (2%)
    pallas_call x1, Pallas kernels, body(): pl.pallas_call(kernel, out_shape=jax.ShapeDtypeStruct((2, 2, 2, 16) + til...  82.9 us
    another operation x1, local copies, waits for them, and re-layouts, body(): result[1].reshape(state_rhs.shape)  1.86 us

profile of v1, /device:TPU:1, one launch (start us, length us, event | category | flops | bytes accessed | tf_op | source)
XLA Modules:
  0.0 85.4 jit_solution(15503631296947278140)
XLA Ops:
  0.6 82.9 %precondition.1 = f32[2,2,2,16,8,128]{5,4,3,2,1,0:T(8,128)} custom-call(f32[2,2,16,8,128]{4,3,2,1,0:T(8,128)} %bitcast.7, f32[2,2,16,8,128]{4,3,2,1,0:T(8,128)} %bitcast.8, f32[2,16,8,128]{3,2,1,0:T(8,128)} %bitcast.9), custom_call_target="tpu_custom_call" | custom-call | tf_op jit(solution)/shard_map/precondition/pallas_call | solution.py:454
  83.5 1.9 %slice_bitcast_fusion = (f32[2,2,128,128]{3,2,1,0:T(8,128)}, f32[2,2,128,128]{3,2,1,0:T(8,128)}) fusion(f32[2,2,2,16,8,128]{5,4,3,2,1,0:T(8,128)} %precondition.1), kind=kLoop, calls=%fused_computation | loop fusion | bytes 1048576 | tf_op jit(solution)/shard_map/reshape;squeeze | solution.py:489

commit v2 on v1

v2 whole, which is shorter than its diff:
```python
import math

import jax
import jax.numpy as jnp
from jax import lax
from jax.experimental import pallas as pl
from jax.experimental.pallas import tpu as pltpu
from jax.sharding import PartitionSpec as P

STEPS = 32
SWEEPS = 12
ALPHA = 0.1
MESH = pl.DeviceIdType.MESH
TAIL = 3
HALO = 8 + TAIL
ROWS = 16 + 2 * HALO
BLOCK = 8
F32 = jnp.float32


def rem(a, n):
    return lax.rem(a, jnp.int32(n))


def div(a, n):
    return lax.div(a, jnp.int32(n))


def mul_const(v, c):
    re, im = v
    cr, ci = c.real, c.imag
    if abs(ci) < 1e-12:
        if abs(cr - 1.0) < 1e-12:
            return v
        return (re * cr, im * cr)
    if abs(cr) < 1e-12:
        if abs(ci - 1.0) < 1e-12:
            return (-im, re)
        if abs(ci + 1.0) < 1e-12:
            return (im, -re)
        return (im * (-ci), re * ci)
    return (re * cr - im * ci, re * ci + im * cr)


def add(a, b):
    return (a[0] + b[0], a[1] + b[1])


def sub(a, b):
    return (a[0] - b[0], a[1] - b[1])


def small_dft(values, sign):
    n = len(values)
    if n == 1:
        return values
    even = small_dft(values[0::2], sign)
    odd = small_dft(values[1::2], sign)
    out = [None] * n
    for k in range(n // 2):
        angle = sign * 2.0 * math.pi * k / n
        t = mul_const(odd[k], complex(math.cos(angle), math.sin(angle)))
        out[k] = add(even[k], t)
        out[k + n // 2] = sub(even[k], t)
    return out


def long_dft(load, store, tmp, sign):
    for b in range(8):
        group = small_dft([load(8 * a + b) for a in range(4)], sign)
        for k1 in range(4):
            angle = sign * 2.0 * math.pi * b * k1 / 32
            re, im = mul_const(group[k1], complex(math.cos(angle), math.sin(angle)))
            tmp[8 * k1 + b, 0] = re
            tmp[8 * k1 + b, 1] = im
    for k1 in range(4):
        group = small_dft([(tmp[8 * k1 + b, 0], tmp[8 * k1 + b, 1]) for b in range(8)], sign)
        for k2 in range(8):
            store(k1 + 4 * k2, group[k2])


def kernel(
    state, adjoint, reaction, out,
    src, rsrc, r1, rf, rha, rhb, b1, tmp, f1, fld, fha, fhb, s, w, u0, u1, g, f2, b2,
    load_sem, send_sem, recv_sem, group_sem,
):
    tm = lax.axis_index("tm")
    sp = lax.axis_index("space")
    x, zlo, core = div(tm, 4), rem(div(tm, 2), 2), rem(tm, 2)
    zhi, y = div(sp, 4), rem(sp, 4)
    z = zhi * 2 + zlo
    zhh, par = div(zhi, 2), rem(zhi, 2)
    zp, rtl = div(x, 2), rem(x, 2)
    freq = x * 8 + y * 2 + core
    home = core == par
    away = jnp.logical_not(home)

    loads = [
        pltpu.make_async_copy(reaction, rsrc, load_sem.at[2]),
        pltpu.make_async_copy(state, src.at[0], load_sem.at[0]),
        pltpu.make_async_copy(adjoint, src.at[1], load_sem.at[1]),
    ]
    for c in loads:
        c.start()

    xs = [rem(x + i, 4) for i in range(4)]
    ys = [rem(y + i, 4) for i in range(4)]
    cs = [core, 1 - core]
    zs = [rem(z + i, 8) for i in range(8)]
    hs = [zhh, 1 - zhh]
    ls = [zlo, 1 - zlo]
    z_tm = [rem(v, 2) * 2 for v in zs]
    z_sp = [div(v, 2) * 4 for v in zs]

    def plane(ix, iz):
        return (xs[ix] * 4 + z_tm[iz] + par, z_sp[iz] + y)

    def mate(ix, iy, ic):
        return (xs[ix] * 4 + zlo * 2 + cs[ic], zhi * 4 + ys[iy])

    def origin(ix, il, ic, h):
        return (xs[ix] * 4 + ls[il] * 2 + cs[ic], (core + 2 * h) * 4 + y)

    above = (x * 4 + z_tm[1] + core, z_sp[1] + y)
    below = (x * 4 + z_tm[7] + core, z_sp[7] + y)
    far_first = (4, 3, 5, 2, 6, 1, 7, 0)
    near_first = (0, 1, 7, 2, 6, 3, 5, 4)
    across = (2, 1, 3, 0)

    def near(cc):
        return div(rem(z - 2 * cc + 9, 8), 4)

    barrier = pltpu.get_barrier_semaphore()

    def greet(dev):
        pl.semaphore_signal(barrier, inc=1, device_id=dev, device_id_type=MESH)

    for iz in far_first:
        for ix in across:
            if ix or iz:
                greet(plane(ix, iz))
    for ih in (1, 0):
        for ix in across:
            for il in (1, 0):
                for ic in (1, 0):
                    if ix or il or ic or ih:
                        greet(origin(ix, il, ic, hs[ih]))
    for iy in across:
        for ix in across:
            for ic in (1, 0):
                if ix or iy or ic:
                    greet(mate(ix, iy, ic))
    greet(above)
    greet(below)

    @pl.when(away)
    def _():
        greet(plane(0, 0))
        greet(origin(0, 0, 0, zhh))

    pl.semaphore_wait(barrier, 97 - 2 * home.astype(jnp.int32))

    def copy_to(src_ref, dst_ref, phase, dev, sem=None):
        return pltpu.make_async_remote_copy(
            src_ref=src_ref, dst_ref=dst_ref, send_sem=send_sem.at[phase],
            recv_sem=recv_sem.at[phase] if sem is None else sem,
            device_id=dev, device_id_type=MESH,
        )

    def wait_on(ref, sem):
        pltpu.make_async_copy(ref, ref, sem).wait()

    def arrived(ref, phase):
        wait_on(ref, recv_sem.at[phase])

    def sent(ref, phase):
        wait_on(ref, send_sem.at[phase])

    loads[0].wait()
    for i in range(2):
        zz = zlo * 4 + core * 2 + i
        tile = rsrc.at[zp, 2 * zz + rtl]
        here = jnp.logical_and(home, zz == z)

        @pl.when(here)
        def _():
            pltpu.make_async_copy(tile, r1.at[zhh], recv_sem.at[0]).start()

        @pl.when(jnp.logical_not(here))
        def _():
            dev = (x * 4 + rem(zz, 2) * 2 + par, div(zz, 2) * 4 + y)
            copy_to(tile, r1.at[zhh], 0, dev).start()

    loads[1].wait()
    loads[2].wait()

    place = b1.at[zhh, :, pl.ds(2 * tm, 2)]
    b1_sem = recv_sem.at[1 + zhh]

    def piece(ix, iz):
        return src.at[:, :, div(xs[ix], 2), 2 * zs[iz] + rem(xs[ix], 2)]

    @pl.when(home)
    def _():
        pltpu.make_async_copy(piece(0, 0), place, b1_sem).start()

    @pl.when(away)
    def _():
        copy_to(piece(0, 0), place, 1, plane(0, 0), b1_sem).start()

    for iz in near_first:
        for ix in across:
            if ix or iz:
                copy_to(piece(ix, iz), place, 1, plane(ix, iz), b1_sem).start()

    arrived(r1, 0)
    pltpu.make_async_copy(r1, rf.at[:, core, y, zp, rtl], recv_sem.at[3]).start()
    for iy in across:
        for ix in across:
            for ic in (1, 0):
                if ix or iy or ic:
                    copy_to(r1, rf.at[:, core, y, zp, rtl], 3, mate(ix, iy, ic)).start()

    def transform(tile):
        def load(n):
            growth = math.exp(math.log(ALPHA) * n / STEPS)
            return (b1[tile, 0, n] * growth, b1[tile, 1, STEPS - 1 - n] * growth)

        def store(k, v):
            f1[k, tile, 0] = v[0]
            f1[k, tile, 1] = v[1]

        long_dft(load, store, tmp, -1)

    def second(tile, half):
        goal = fld.at[tile, core, y, zp, rtl]
        for iy in across:
            for ix in across:
                for ic in (1, 0):
                    if ix or iy or ic:
                        k = xs[ix] * 8 + ys[iy] * 2 + cs[ic]
                        copy_to(f1.at[k, tile], goal, 4, mate(ix, iy, ic), group_sem.at[half, iy]).start()
        pltpu.make_async_copy(f1.at[freq, tile], goal, group_sem.at[half, 0]).start()

    def pass_on(half):
        for iy in across:
            yy = ys[(4 - iy) % 4]
            wait_on(fld.at[0, :, yy], group_sem.at[half, iy])
            for cc in range(2):
                tile = near(cc) if half == 0 else 1 - near(cc)
                at = (tile, cc, yy)
                got = fld.at[at]
                copy_to(got.at[:, 0], fha.at[(1,) + at], 5, below).start()
                copy_to(got.at[:, 1], fha.at[(0,) + at], 6, above).start()
                copy_to(got.at[:, 1, :, pl.ds(0, TAIL)], fhb.at[(1,) + at].at[:, :, :TAIL], 7, below).start()
                copy_to(got.at[:, 0, :, pl.ds(8 - TAIL, TAIL)], fhb.at[(0,) + at].at[:, :, :TAIL], 8, above).start()

    close = near(core)
    arrived(b1.at[0], 1 + close)
    transform(close)
    second(close, 0)

    arrived(rf, 3)
    cos_k, sin_k = jnp.float32(0.0), jnp.float32(0.0)
    for k in range(STEPS):
        angle = 2.0 * math.pi * k / STEPS
        cos_k = jnp.where(freq == k, jnp.float32(math.cos(angle)), cos_k)
        sin_k = jnp.where(freq == k, jnp.float32(math.sin(angle)), sin_k)
    rate = math.exp(math.log(ALPHA) / STEPS)
    base_re = 1.0 - rate * cos_k + 6.0
    d_im = rate * sin_k + 1.0

    def coefficient(row, j, value, keep):
        d_re = base_re + value
        inv = 1.0 / (d_re * d_re + d_im * d_im)
        w_re = d_re * inv
        w_im = -d_im * inv
        if keep is not None:
            w_re = jnp.where(keep, w_re, 0.0)
            w_im = jnp.where(keep, w_im, 0.0)
        w[row, 0, j] = w_re
        w[row, 1, j] = w_im

    rfl = rf.reshape(512, 128)
    ral = rha.reshape(512, 128)
    rbl = rhb.reshape(512, 128)

    def inner_rows(r, _):
        for t in range(2):
            for j in range(4):
                value = rfl[pl.ds(j * 16 + t * 8 + r, 8, stride=64), :]
                coefficient(HALO + t * 8 + r, j, value, None)
        return 0

    lax.fori_loop(0, 8, inner_rows, 0)

    arrived(b1.at[0], 2 - close)
    transform(1 - close)
    second(1 - close, 1)
    copy_to(rf.at[:, :, :, :, 0], rha.at[1], 9, below).start()
    copy_to(rf.at[:, :, :, :, 1], rha.at[0], 10, above).start()
    copy_to(rf.at[:, :, :, :, 1, pl.ds(0, TAIL)], rhb.at[1, :, :, :, :, :TAIL], 11, below).start()
    copy_to(rf.at[:, :, :, :, 0, pl.ds(8 - TAIL, TAIL)], rhb.at[0, :, :, :, :, :TAIL], 12, above).start()
    pass_on(0)
    for side in range(2):
        arrived(rha.at[side], 10 - side)
        arrived(rhb.at[side, :, :, :, :, :TAIL], 12 - side)

    def outer_rows(side, r, at, flat):
        keep = (z > 0) if side == 0 else (z < 7)
        for j in range(4):
            value = flat[pl.ds(side * 256 + j * 8 + at, 8, stride=32), :]
            coefficient(r, j, value, keep)

    def wide_rows(r, _):
        outer_rows(0, TAIL + r, r, ral)
        outer_rows(1, HALO + 16 + r, r, ral)
        return 0

    lax.fori_loop(0, 8, wide_rows, 0)
    for r in range(TAIL):
        outer_rows(0, r, r, rbl)
        outer_rows(1, HALO + 24 + r, r, rbl)

    pass_on(1)

    fll = fld.reshape(1024, 128)
    fal = fha.reshape(1024, 128)
    fbl = fhb.reshape(1024, 128)

    def start_row(row, j, v):
        s[row, 0, j] = v[0]
        s[row, 1, j] = v[1]
        w_re, w_im = w[row, 0, j], w[row, 1, j]
        u0[row, 0, j] = w_re * v[0] - w_im * v[1]
        u0[row, 1, j] = w_re * v[1] + w_im * v[0]

    def inner_start(r, _):
        for t in range(2):
            for j in range(4):
                v = [fll[pl.ds(j * 32 + t * 16 + c * 8 + r, 8, stride=128), :] for c in range(2)]
                start_row(HALO + t * 8 + r, j, v)
        return 0

    lax.fori_loop(0, 8, inner_start, 0)
    for side in range(2):
        arrived(fha.at[side], 6 - side)
        arrived(fhb.at[side, :, :, :, :, :, :TAIL], 8 - side)

    def outer_start(side, row, at, flat):
        for j in range(4):
            first = side * 512 + j * 16 + at
            v = [flat[pl.ds(first + c * 8, 8, stride=64), :] for c in range(2)]
            start_row(row, j, v)

    def wide_start(r, _):
        outer_start(0, TAIL + r, r, fal)
        outer_start(1, HALO + 16 + r, r, fal)
        return 0

    lax.fori_loop(0, 8, wide_start, 0)
    for r in range(TAIL):
        outer_start(0, r, r, fbl)
        outer_start(1, HALO + 24 + r, r, fbl)

    lanes = lax.broadcasted_iota(jnp.int32, (8, 128), 1)
    subs = lax.broadcasted_iota(jnp.int32, (8, 128), 0)
    first_lane, last_lane = lanes == 0, lanes == 127
    first_sub, last_sub = subs == 0, subs == 7

    def sweep_row(old, new, row):
        total = [[None] * 4, [None] * 4]
        for c in range(2):
            mid = [old[row, c, j] for j in range(4)]
            before = jnp.where(first_sub, 0.0, pltpu.roll(mid[3], 1, 0))
            after = jnp.where(last_sub, 0.0, pltpu.roll(mid[0], 7, 0))
            line = [before] + mid + [after]
            for j in range(4):
                t = s[row, c, j] + (line[j] + line[j + 2])
                t = t + (old[row - 1, c, j] + old[row + 1, c, j])
                left = jnp.where(first_lane, 0.0, pltpu.roll(mid[j], 1, 1))
                right = jnp.where(last_lane, 0.0, pltpu.roll(mid[j], 127, 1))
                total[c][j] = t + (left + right)
        for j in range(4):
            w_re, w_im = w[row, 0, j], w[row, 1, j]
            t_re, t_im = total[0][j], total[1][j]
            new[row, 0, j] = w_re * t_re - w_im * t_im
            new[row, 1, j] = w_re * t_im + w_im * t_re

    def sweep(old, new, low, high):
        count = high - low

        def block(i, _):
            start = jnp.minimum(low + BLOCK * i, high - BLOCK)
            for k in range(BLOCK):
                sweep_row(old, new, start + k)
            return 0

        lax.fori_loop(0, (count + BLOCK - 1) // BLOCK, block, 0)

    pair = [u0, u1]
    for m in range(1, SWEEPS):
        sweep(pair[(m + 1) % 2], pair[m % 2], m, ROWS - m)
    result = pair[(SWEEPS - 1) % 2]

    gl = g.reshape(1024, 128)

    def turn_back(r, _):
        for t in range(2):
            for j in range(4):
                for c in range(2):
                    gl[pl.ds(j * 32 + t * 16 + c * 8 + r, 8, stride=128), :] = result[HALO + t * 8 + r, c, j]
        return 0

    lax.fori_loop(0, 8, turn_back, 0)

    for half in range(2):
        tiles = [1 - near(cc) if half == 0 else near(cc) for cc in cs]
        for iy in across:
            for ix in across:
                for ic in (1, 0):
                    if ix or iy or ic:
                        part = g.at[tiles[ic], cs[ic], ys[iy], div(xs[ix], 2), rem(xs[ix], 2)]
                        copy_to(part, f2.at[tiles[ic], freq], 13, mate(ix, iy, ic), recv_sem.at[14 + half]).start()
        own = g.at[tiles[0], core, y, zp, rtl]
        pltpu.make_async_copy(own, f2.at[tiles[0], freq], recv_sem.at[14 + half]).start()

    def transform_back(tile):
        def load(k):
            return (f2[tile, k, 0], f2[tile, k, 1])

        def store(n, v):
            shrink = math.exp(-math.log(ALPHA) * n / STEPS) / STEPS
            b2[tile, 0, n] = v[0] * shrink
            b2[tile, 1, STEPS - 1 - n] = v[1] * shrink

        long_dft(load, store, tmp, 1)

    goal = out.at[:, :, zp, 2 * z + rtl]

    def fourth(tile):
        for ix in across:
            for il in (1, 0):
                for ic in (1, 0):
                    times = pl.ds(2 * (xs[ix] * 4 + ls[il] * 2 + cs[ic]), 2)
                    part = b2.at[tile, :, times]
                    dev = origin(ix, il, ic, tile)
                    if ix or il or ic:
                        copy_to(part, goal, 16, dev).start()
                    else:
                        here = jnp.logical_and(home, tile == zhh)

                        @pl.when(here)
                        def _():
                            pltpu.make_async_copy(part, goal, recv_sem.at[16]).start()

                        @pl.when(jnp.logical_not(here))
                        def _():
                            copy_to(part, goal, 16, dev).start()

    arrived(f2.at[0], 14)
    transform_back(1 - close)
    fourth(1 - close)
    arrived(f2.at[0], 15)
    transform_back(close)
    fourth(close)

    for i in range(2):
        zz = zlo * 4 + core * 2 + i

        @pl.when(jnp.logical_not(jnp.logical_and(home, zz == z)))
        def _():
            sent(r1.at[0], 0)

    for side in range(2):
        sent(fha.at[side], 6 - side)
        sent(fhb.at[side, :, :, :, :, :, :TAIL], 8 - side)
        sent(rha.at[side], 10 - side)
        sent(rhb.at[side, :, :, :, :, :TAIL], 12 - side)

    def drain(i, _):
        sent(b1.at[0, :, pl.ds(0, 2)], 1)
        sent(r1, 3)
        sent(f1.at[0], 4)
        sent(f1.at[0], 13)
        sent(b1.at[0, :, pl.ds(0, 2)], 16)
        return 0

    lax.fori_loop(1, 32, drain, 0)

    @pl.when(away)
    def _():
        sent(b1.at[0, :, pl.ds(0, 2)], 1)
        sent(b1.at[0, :, pl.ds(0, 2)], 16)

    arrived(out, 16)


def body(state_rhs, adjoint_rhs, reaction):
    tile = (8, 128)
    planes = (2, 2, 4, 2)
    field = pltpu.VMEM((ROWS, 2, 4) + tile, F32)
    result = pl.pallas_call(
        kernel,
        out_shape=jax.ShapeDtypeStruct((2, 2, 2, 16) + tile, F32),
        in_specs=[pl.BlockSpec(memory_space=pl.ANY)] * 3,
        out_specs=pl.BlockSpec(memory_space=pl.ANY),
        scratch_shapes=[
            pltpu.VMEM((2, 2, 2, 16) + tile, F32),
            pltpu.VMEM((2, 16) + tile, F32),
            pltpu.VMEM((2,) + tile, F32),
            pltpu.VMEM(planes + (2,) + tile, F32),
            pltpu.VMEM((2,) + planes + tile, F32),
            pltpu.VMEM((2,) + planes + tile, F32),
            pltpu.VMEM((2, 2, 32) + tile, F32),
            pltpu.VMEM((32, 2) + tile, F32),
            pltpu.VMEM((32, 2, 2) + tile, F32),
            pltpu.VMEM(planes + (2, 2) + tile, F32),
            pltpu.VMEM((2,) + planes + (2,) + tile, F32),
            pltpu.VMEM((2,) + planes + (2,) + tile, F32),
            field,
            field,
            field,
            field,
            pltpu.VMEM(planes + (2, 2) + tile, F32),
            pltpu.VMEM((2, 32, 2) + tile, F32),
            pltpu.VMEM((2, 2, 32) + tile, F32),
            pltpu.SemaphoreType.DMA((3,)),
            pltpu.SemaphoreType.DMA((17,)),
            pltpu.SemaphoreType.DMA((17,)),
            pltpu.SemaphoreType.DMA((2, 4)),
        ],
        compiler_params=pltpu.CompilerParams(collective_id=0, has_side_effects=True),
        name="precondition",
    )(
        state_rhs.reshape((2, 2, 16) + tile),
        adjoint_rhs.reshape((2, 2, 16) + tile),
        reaction.reshape((2, 16) + tile),
    )
    return (result[0].reshape(state_rhs.shape), result[1].reshape(state_rhs.shape))


def solution(mesh):
    placed = P("tm", "space", None, None)
    return jax.shard_map(
        body,
        mesh=mesh,
        in_specs=(placed, placed, P("space", None, None)),
        out_specs=(placed, placed),
        check_vma=False,
    )
```

time: 85.5 us -> 71.5 us (0.84)
  Pallas kernels: 82.9 us -> 68.9 us
    pallas_call x1, Pallas kernels: 82.9 us -> 68.9 us  [body(): pl.pallas_call(kernel, out_shape=jax.ShapeDtypeStruct((2, 2, 2, 16) + til...]
where the time goes in v2:
time: 71.5 us; the launch traced here: 71.4 us
  Pallas kernels  68.9 us (96%)
  local copies, waits for them, and re-layouts  1.86 us (3%)
    pallas_call x1, Pallas kernels, body(): pl.pallas_call(kernel, out_shape=jax.ShapeDtypeStruct((2, 2, 2, 16) + til...  68.9 us
    another operation x1, local copies, waits for them, and re-layouts, body(): result[1].reshape(state_rhs.shape)  1.86 us

profile of v2, /device:TPU:1, one launch (start us, length us, event | category | flops | bytes accessed | tf_op | source)
XLA Modules:
  0.0 71.4 jit_solution(1283220135796581273)
XLA Ops:
  0.6 68.9 %precondition.1 = f32[2,2,2,16,8,128]{5,4,3,2,1,0:T(8,128)} custom-call(f32[2,2,16,8,128]{4,3,2,1,0:T(8,128)} %bitcast.7, f32[2,2,16,8,128]{4,3,2,1,0:T(8,128)} %bitcast.8, f32[2,16,8,128]{3,2,1,0:T(8,128)} %bitcast.9), custom_call_target="tpu_custom_call" | custom-call | tf_op jit(solution)/shard_map/precondition/pallas_call | solution.py:503
  69.5 1.9 %slice_bitcast_fusion = (f32[2,2,128,128]{3,2,1,0:T(8,128)}, f32[2,2,128,128]{3,2,1,0:T(8,128)}) fusion(f32[2,2,2,16,8,128]{5,4,3,2,1,0:T(8,128)} %precondition.1), kind=kLoop, calls=%fused_computation | loop fusion | bytes 1048576 | tf_op jit(solution)/shard_map/reshape;squeeze | solution.py:540

commit v3 on v2

--- a/solution.py
+++ b/solution.py
@@ -14,7 +14,6 @@
 TAIL = 3
 HALO = 8 + TAIL
 ROWS = 16 + 2 * HALO
-BLOCK = 8
 F32 = jnp.float32
 
 
@@ -81,7 +80,7 @@
 
 def kernel(
     state, adjoint, reaction, out,
-    src, rsrc, r1, rf, rha, rhb, b1, tmp, f1, fld, fha, fhb, s, w, u0, u1, g, f2, b2,
+    src, rsrc, r1, rf, b1, tmp, f1, fld, fha, fhb, s, w, u, g, f2, b2,
     load_sem, send_sem, recv_sem, group_sem,
 ):
     tm = lax.axis_index("tm")
@@ -90,13 +89,15 @@
     zhi, y = div(sp, 4), rem(sp, 4)
     z = zhi * 2 + zlo
     zhh, par = div(zhi, 2), rem(zhi, 2)
-    zp, rtl = div(x, 2), rem(x, 2)
+    zp, rtl = rem(x, 2), div(x, 2)
     freq = x * 8 + y * 2 + core
     home = core == par
     away = jnp.logical_not(home)
 
     loads = [
-        pltpu.make_async_copy(reaction, rsrc, load_sem.at[2]),
+        pltpu.make_async_copy(reaction, rsrc.at[:, 2:18], load_sem.at[2]),
+        pltpu.make_async_copy(reaction.at[:, 14:16], rsrc.at[:, 0:2], load_sem.at[3]),
+        pltpu.make_async_copy(reaction.at[:, 0:2], rsrc.at[:, 18:20], load_sem.at[4]),
         pltpu.make_async_copy(state, src.at[0], load_sem.at[0]),
         pltpu.make_async_copy(adjoint, src.at[1], load_sem.at[1]),
     ]
@@ -176,29 +177,30 @@
     def sent(ref, phase):
         wait_on(ref, send_sem.at[phase])
 
-    loads[0].wait()
+    for c in loads[:3]:
+        c.wait()
     for i in range(2):
         zz = zlo * 4 + core * 2 + i
-        tile = rsrc.at[zp, 2 * zz + rtl]
         here = jnp.logical_and(home, zz == z)
+        rows = rsrc.at[zp, pl.ds(2 * zz, 6)]
 
         @pl.when(here)
         def _():
-            pltpu.make_async_copy(tile, r1.at[zhh], recv_sem.at[0]).start()
+            pltpu.make_async_copy(rows, r1.at[zhh], recv_sem.at[0]).start()
 
         @pl.when(jnp.logical_not(here))
         def _():
             dev = (x * 4 + rem(zz, 2) * 2 + par, div(zz, 2) * 4 + y)
-            copy_to(tile, r1.at[zhh], 0, dev).start()
-
-    loads[1].wait()
-    loads[2].wait()
+            copy_to(rows, r1.at[zhh], 0, dev).start()
+
+    for c in loads[3:]:
+        c.wait()
 
     place = b1.at[zhh, :, pl.ds(2 * tm, 2)]
     b1_sem = recv_sem.at[1 + zhh]
 
     def piece(ix, iz):
-        return src.at[:, :, div(xs[ix], 2), 2 * zs[iz] + rem(xs[ix], 2)]
+        return src.at[:, :, rem(xs[ix], 2), 2 * zs[iz] + div(xs[ix], 2)]
 
     @pl.when(home)
     def _():
@@ -212,14 +214,6 @@
         for ix in across:
             if ix or iz:
                 copy_to(piece(ix, iz), place, 1, plane(ix, iz), b1_sem).start()
-
-    arrived(r1, 0)
-    pltpu.make_async_copy(r1, rf.at[:, core, y, zp, rtl], recv_sem.at[3]).start()
-    for iy in across:
-        for ix in across:
-            for ic in (1, 0):
-                if ix or iy or ic:
-                    copy_to(r1, rf.at[:, core, y, zp, rtl], 3, mate(ix, iy, ic)).start()
 
     def transform(tile):
         def load(n):
@@ -242,25 +236,49 @@
                         copy_to(f1.at[k, tile], goal, 4, mate(ix, iy, ic), group_sem.at[half, iy]).start()
         pltpu.make_async_copy(f1.at[freq, tile], goal, group_sem.at[half, 0]).start()
 
+    def shared(half, iy):
+        yy = ys[(4 - iy) % 4]
+        for cc in range(2):
+            tile = near(cc) if half == 0 else 1 - near(cc)
+            yield (tile, cc, yy)
+
     def pass_on(half):
         for iy in across:
-            yy = ys[(4 - iy) % 4]
-            wait_on(fld.at[0, :, yy], group_sem.at[half, iy])
-            for cc in range(2):
-                tile = near(cc) if half == 0 else 1 - near(cc)
-                at = (tile, cc, yy)
+            wait_on(fld.at[0, :, ys[(4 - iy) % 4]], group_sem.at[half, iy])
+            for at in shared(half, iy):
                 got = fld.at[at]
                 copy_to(got.at[:, 0], fha.at[(1,) + at], 5, below).start()
                 copy_to(got.at[:, 1], fha.at[(0,) + at], 6, above).start()
-                copy_to(got.at[:, 1, :, pl.ds(0, TAIL)], fhb.at[(1,) + at].at[:, :, :TAIL], 7, below).start()
-                copy_to(got.at[:, 0, :, pl.ds(8 - TAIL, TAIL)], fhb.at[(0,) + at].at[:, :, :TAIL], 8, above).start()
+
+    def pass_rest():
+        for half in range(2):
+            for iy in across:
+                for at in shared(half, iy):
+                    got = fld.at[at]
+                    copy_to(got.at[:, 1, :, pl.ds(0, TAIL)], fhb.at[(1,) + at].at[:, :, :TAIL], 7, below).start()
+                    copy_to(got.at[:, 0, :, pl.ds(8 - TAIL, TAIL)], fhb.at[(0,) + at].at[:, :, :TAIL], 8, above).start()
+
+    arrived(r1, 0)
+    half_rf = rf.at[:, core]
+    beside = rem(x + 1 + 2 * rem(y, 2), 4)
+    for iy in across:
+        copy_to(r1, half_rf.at[:, y, zp], 3, (beside * 4 + zlo * 2 + core, zhi * 4 + ys[iy])).start()
+    for iy in across[:3]:
+        copy_to(r1, half_rf.at[:, y, zp], 3, mate(0, iy, 0)).start()
+    pltpu.make_async_copy(r1, half_rf.at[:, y, zp], recv_sem.at[3]).start()
 
     close = near(core)
     arrived(b1.at[0], 1 + close)
     transform(close)
     second(close, 0)
 
-    arrived(rf, 3)
+    arrived(rf.at[:, 0], 3)
+    copy_to(half_rf, half_rf, 9, mate(0, 0, 1)).start()
+    arrived(b1.at[0], 2 - close)
+    transform(1 - close)
+    second(1 - close, 1)
+    pass_on(0)
+    arrived(rf.at[:, 0], 9)
     cos_k, sin_k = jnp.float32(0.0), jnp.float32(0.0)
     for k in range(STEPS):
         angle = 2.0 * math.pi * k / STEPS
@@ -281,48 +299,27 @@
         w[row, 0, j] = w_re
         w[row, 1, j] = w_im
 
-    rfl = rf.reshape(512, 128)
-    ral = rha.reshape(512, 128)
-    rbl = rhb.reshape(512, 128)
-
-    def inner_rows(r, _):
-        for t in range(2):
-            for j in range(4):
-                value = rfl[pl.ds(j * 16 + t * 8 + r, 8, stride=64), :]
-                coefficient(HALO + t * 8 + r, j, value, None)
+    rfl = rf.reshape(1536, 128)
+
+    def coefficient_row(row, keep):
+        for j in range(4):
+            value = rfl[pl.ds(j * 48 + row + 16 - HALO, 8, stride=192), :]
+            coefficient(row, j, value, keep)
+
+    def coefficient_rows(r, _):
+        coefficient_row(HALO + r, None)
+        coefficient_row(HALO + 8 + r, None)
+        coefficient_row(TAIL + r, z > 0)
+        coefficient_row(HALO + 16 + r, z < 7)
         return 0
 
-    lax.fori_loop(0, 8, inner_rows, 0)
-
-    arrived(b1.at[0], 2 - close)
-    transform(1 - close)
-    second(1 - close, 1)
-    copy_to(rf.at[:, :, :, :, 0], rha.at[1], 9, below).start()
-    copy_to(rf.at[:, :, :, :, 1], rha.at[0], 10, above).start()
-    copy_to(rf.at[:, :, :, :, 1, pl.ds(0, TAIL)], rhb.at[1, :, :, :, :, :TAIL], 11, below).start()
-    copy_to(rf.at[:, :, :, :, 0, pl.ds(8 - TAIL, TAIL)], rhb.at[0, :, :, :, :, :TAIL], 12, above).start()
-    pass_on(0)
-    for side in range(2):
-        arrived(rha.at[side], 10 - side)
-        arrived(rhb.at[side, :, :, :, :, :TAIL], 12 - side)
-
-    def outer_rows(side, r, at, flat):
-        keep = (z > 0) if side == 0 else (z < 7)
-        for j in range(4):
-            value = flat[pl.ds(side * 256 + j * 8 + at, 8, stride=32), :]
-            coefficient(r, j, value, keep)
-
-    def wide_rows(r, _):
-        outer_rows(0, TAIL + r, r, ral)
-        outer_rows(1, HALO + 16 + r, r, ral)
-        return 0
-
-    lax.fori_loop(0, 8, wide_rows, 0)
+    lax.fori_loop(0, 8, coefficient_rows, 0)
     for r in range(TAIL):
-        outer_rows(0, r, r, rbl)
-        outer_rows(1, HALO + 24 + r, r, rbl)
+        coefficient_row(r, z > 0)
+        coefficient_row(HALO + 24 + r, z < 7)
 
     pass_on(1)
+    pass_rest()
 
     fll = fld.reshape(1024, 128)
     fal = fha.reshape(1024, 128)
@@ -332,8 +329,8 @@
         s[row, 0, j] = v[0]
         s[row, 1, j] = v[1]
         w_re, w_im = w[row, 0, j], w[row, 1, j]
-        u0[row, 0, j] = w_re * v[0] - w_im * v[1]
-        u0[row, 1, j] = w_re * v[1] + w_im * v[0]
+        u[0, row, 0, j] = w_re * v[0] - w_im * v[1]
+        u[0, row, 1, j] = w_re * v[1] + w_im * v[0]
 
     def inner_start(r, _):
         for t in range(2):
@@ -343,65 +340,62 @@
         return 0
 
     lax.fori_loop(0, 8, inner_start, 0)
-    for side in range(2):
-        arrived(fha.at[side], 6 - side)
-        arrived(fhb.at[side, :, :, :, :, :, :TAIL], 8 - side)
-
-    def outer_start(side, row, at, flat):
-        for j in range(4):
-            first = side * 512 + j * 16 + at
-            v = [flat[pl.ds(first + c * 8, 8, stride=64), :] for c in range(2)]
-            start_row(row, j, v)
-
-    def wide_start(r, _):
-        outer_start(0, TAIL + r, r, fal)
-        outer_start(1, HALO + 16 + r, r, fal)
-        return 0
-
-    lax.fori_loop(0, 8, wide_start, 0)
-    for r in range(TAIL):
-        outer_start(0, r, r, fbl)
-        outer_start(1, HALO + 24 + r, r, fbl)
-
     lanes = lax.broadcasted_iota(jnp.int32, (8, 128), 1)
     subs = lax.broadcasted_iota(jnp.int32, (8, 128), 0)
     first_lane, last_lane = lanes == 0, lanes == 127
     first_sub, last_sub = subs == 0, subs == 7
 
-    def sweep_row(old, new, row):
+    def sweep_row(m, row):
         total = [[None] * 4, [None] * 4]
         for c in range(2):
-            mid = [old[row, c, j] for j in range(4)]
+            mid = [u[m - 1, row, c, j] for j in range(4)]
             before = jnp.where(first_sub, 0.0, pltpu.roll(mid[3], 1, 0))
             after = jnp.where(last_sub, 0.0, pltpu.roll(mid[0], 7, 0))
             line = [before] + mid + [after]
             for j in range(4):
                 t = s[row, c, j] + (line[j] + line[j + 2])
-                t = t + (old[row - 1, c, j] + old[row + 1, c, j])
+                t = t + (u[m - 1, row - 1, c, j] + u[m - 1, row + 1, c, j])
                 left = jnp.where(first_lane, 0.0, pltpu.roll(mid[j], 1, 1))
                 right = jnp.where(last_lane, 0.0, pltpu.roll(mid[j], 127, 1))
                 total[c][j] = t + (left + right)
         for j in range(4):
             w_re, w_im = w[row, 0, j], w[row, 1, j]
             t_re, t_im = total[0][j], total[1][j]
-            new[row, 0, j] = w_re * t_re - w_im * t_im
-            new[row, 1, j] = w_re * t_im + w_im * t_re
-
-    def sweep(old, new, low, high):
-        count = high - low
-
-        def block(i, _):
-            start = jnp.minimum(low + BLOCK * i, high - BLOCK)
-            for k in range(BLOCK):
-                sweep_row(old, new, start + k)
-            return 0
-
-        lax.fori_loop(0, (count + BLOCK - 1) // BLOCK, block, 0)
-
-    pair = [u0, u1]
-    for m in range(1, SWEEPS):
-        sweep(pair[(m + 1) % 2], pair[m % 2], m, ROWS - m)
-    result = pair[(SWEEPS - 1) % 2]
+            u[m, row, 0, j] = w_re * t_re - w_im * t_im
+            u[m, row, 1, j] = w_re * t_im + w_im * t_re
+
+    done = [set() for _ in range(SWEEPS)]
+
+    def sweeps(edge):
+        for m in range(1, SWEEPS):
+            rows = set(range(edge + m, ROWS - edge - m)) - done[m]
+            done[m] |= rows
+            for row in sorted(rows):
+                sweep_row(m, row)
+
+    sweeps(HALO)
+    for side in range(2):
+        arrived(fha.at[side], 6 - side)
+
+    def outer_start(side, row, at, flat):
+        for j in range(4):
+            first = side * 512 + j * 16 + at
+            v = [flat[pl.ds(first + c * 8, 8, stride=64), :] for c in range(2)]
+            start_row(row, j, v)
+
+    def wide_start(r, _):
+        outer_start(0, TAIL + r, r, fal)
+        outer_start(1, HALO + 16 + r, r, fal)
+        return 0
+
+    lax.fori_loop(0, 8, wide_start, 0)
+    sweeps(TAIL)
+    for side in range(2):
+        arrived(fhb.at[side, :, :, :, :, :, :TAIL], 8 - side)
+    for r in range(TAIL):
+        outer_start(0, r, r, fbl)
+        outer_start(1, HALO + 24 + r, r, fbl)
+    sweeps(0)
 
     gl = g.reshape(1024, 128)
 
@@ -409,7 +403,7 @@
         for t in range(2):
             for j in range(4):
                 for c in range(2):
-                    gl[pl.ds(j * 32 + t * 16 + c * 8 + r, 8, stride=128), :] = result[HALO + t * 8 + r, c, j]
+                    gl[pl.ds(j * 32 + t * 16 + c * 8 + r, 8, stride=128), :] = u[SWEEPS - 1, HALO + t * 8 + r, c, j]
         return 0
 
     lax.fori_loop(0, 8, turn_back, 0)
@@ -420,7 +414,7 @@
             for ix in across:
                 for ic in (1, 0):
                     if ix or iy or ic:
-                        part = g.at[tiles[ic], cs[ic], ys[iy], div(xs[ix], 2), rem(xs[ix], 2)]
+                        part = g.at[tiles[ic], cs[ic], ys[iy], rem(xs[ix], 2), div(xs[ix], 2)]
                         copy_to(part, f2.at[tiles[ic], freq], 13, mate(ix, iy, ic), recv_sem.at[14 + half]).start()
         own = g.at[tiles[0], core, y, zp, rtl]
         pltpu.make_async_copy(own, f2.at[tiles[0], freq], recv_sem.at[14 + half]).start()
@@ -475,12 +469,17 @@
     for side in range(2):
         sent(fha.at[side], 6 - side)
         sent(fhb.at[side, :, :, :, :, :, :TAIL], 8 - side)
-        sent(rha.at[side], 10 - side)
-        sent(rhb.at[side, :, :, :, :, :TAIL], 12 - side)
+
+    sent(rf.at[:, 0], 9)
+
+    def drain_reaction(i, _):
+        sent(r1, 3)
+        return 0
+
+    lax.fori_loop(1, 8, drain_reaction, 0)
 
     def drain(i, _):
         sent(b1.at[0, :, pl.ds(0, 2)], 1)
-        sent(r1, 3)
         sent(f1.at[0], 4)
         sent(f1.at[0], 13)
         sent(b1.at[0, :, pl.ds(0, 2)], 16)
@@ -507,11 +506,9 @@
         out_specs=pl.BlockSpec(memory_space=pl.ANY),
         scratch_shapes=[
             pltpu.VMEM((2, 2, 2, 16) + tile, F32),
-            pltpu.VMEM((2, 16) + tile, F32),
-            pltpu.VMEM((2,) + tile, F32),
-            pltpu.VMEM(planes + (2,) + tile, F32),
-            pltpu.VMEM((2,) + planes + tile, F32),
-            pltpu.VMEM((2,) + planes + tile, F32),
+            pltpu.VMEM((2, 20) + tile, F32),
+            pltpu.VMEM((2, 6) + tile, F32),
+            pltpu.VMEM(planes + (6,) + tile, F32),
             pltpu.VMEM((2, 2, 32) + tile, F32),
             pltpu.VMEM((32, 2) + tile, F32),
             pltpu.VMEM((32, 2, 2) + tile, F32),
@@ -520,12 +517,11 @@
             pltpu.VMEM((2,) + planes + (2,) + tile, F32),
             field,
             field,
-            field,
-            field,
+            pltpu.VMEM((SWEEPS, ROWS, 2, 4) + tile, F32),
             pltpu.VMEM(planes + (2, 2) + tile, F32),
             pltpu.VMEM((2, 32, 2) + tile, F32),
             pltpu.VMEM((2, 2, 32) + tile, F32),
-            pltpu.SemaphoreType.DMA((3,)),
+            pltpu.SemaphoreType.DMA((5,)),
             pltpu.SemaphoreType.DMA((17,)),
             pltpu.SemaphoreType.DMA((17,)),
             pltpu.SemaphoreType.DMA((2, 4)),

time: 71.5 us -> 66.5 us (0.930)
  Pallas kernels: 68.9 us -> 63.9 us
    pallas_call x1, Pallas kernels: 68.9 us -> 63.9 us  [body(): pl.pallas_call(kernel, out_shape=jax.ShapeDtypeStruct((2, 2, 2, 16) + til...]
where the time goes in v3:
time: 66.5 us; the launch traced here: 66.4 us
  Pallas kernels  63.9 us (96%)
  local copies, waits for them, and re-layouts  1.86 us (3%)
    pallas_call x1, Pallas kernels, body(): pl.pallas_call(kernel, out_shape=jax.ShapeDtypeStruct((2, 2, 2, 16) + til...  63.9 us
    another operation x1, local copies, waits for them, and re-layouts, body(): result[1].reshape(state_rhs.shape)  1.86 us

profile of v3, /device:TPU:1, one launch (start us, length us, event | category | flops | bytes accessed | tf_op | source)
XLA Modules:
  0.0 66.4 jit_solution(9014317578432642917)
XLA Ops:
  0.6 63.9 %precondition.1 = f32[2,2,2,16,8,128]{5,4,3,2,1,0:T(8,128)} custom-call(f32[2,2,16,8,128]{4,3,2,1,0:T(8,128)} %bitcast.7, f32[2,2,16,8,128]{4,3,2,1,0:T(8,128)} %bitcast.8, f32[2,16,8,128]{3,2,1,0:T(8,128)} %bitcast.9), custom_call_target="tpu_custom_call" | custom-call | tf_op jit(solution)/shard_map/precondition/pallas_call | solution.py:502
  64.5 1.9 %slice_bitcast_fusion = (f32[2,2,128,128]{3,2,1,0:T(8,128)}, f32[2,2,128,128]{3,2,1,0:T(8,128)}) fusion(f32[2,2,2,16,8,128]{5,4,3,2,1,0:T(8,128)} %precondition.1), kind=kLoop, calls=%fused_computation | loop fusion | bytes 1048576 | tf_op jit(solution)/shard_map/reshape;squeeze | solution.py:536

commit v4 on v3

--- a/solution.py
+++ b/solution.py
@@ -243,7 +243,7 @@
             yield (tile, cc, yy)
 
     def pass_on(half):
-        for iy in across:
+        for iy in (0, 1, 3, 2):
             wait_on(fld.at[0, :, ys[(4 - iy) % 4]], group_sem.at[half, iy])
             for at in shared(half, iy):
                 got = fld.at[at]

time: 66.5 us -> 65.3 us (0.982)
  Pallas kernels: 63.9 us -> 62.6 us
    pallas_call x1, Pallas kernels: 63.9 us -> 62.6 us  [body(): pl.pallas_call(kernel, out_shape=jax.ShapeDtypeStruct((2, 2, 2, 16) + til...]
where the time goes in v4:
time: 65.3 us; the launch traced here: 65.1 us
  Pallas kernels  62.6 us (96%)
  local copies, waits for them, and re-layouts  1.86 us (3%)
    pallas_call x1, Pallas kernels, body(): pl.pallas_call(kernel, out_shape=jax.ShapeDtypeStruct((2, 2, 2, 16) + til...  62.6 us
    another operation x1, local copies, waits for them, and re-layouts, body(): result[1].reshape(state_rhs.shape)  1.86 us

profile of v4, /device:TPU:1, one launch (start us, length us, event | category | flops | bytes accessed | tf_op | source)
XLA Modules:
  0.0 65.1 jit_solution(15035887700125075690)
XLA Ops:
  0.6 62.6 %precondition.1 = f32[2,2,2,16,8,128]{5,4,3,2,1,0:T(8,128)} custom-call(f32[2,2,16,8,128]{4,3,2,1,0:T(8,128)} %bitcast.7, f32[2,2,16,8,128]{4,3,2,1,0:T(8,128)} %bitcast.8, f32[2,16,8,128]{3,2,1,0:T(8,128)} %bitcast.9), custom_call_target="tpu_custom_call" | custom-call | tf_op jit(solution)/shard_map/precondition/pallas_call | solution.py:502
  63.2 1.9 %slice_bitcast_fusion = (f32[2,2,128,128]{3,2,1,0:T(8,128)}, f32[2,2,128,128]{3,2,1,0:T(8,128)}) fusion(f32[2,2,2,16,8,128]{5,4,3,2,1,0:T(8,128)} %precondition.1), kind=kLoop, calls=%fused_computation | loop fusion | bytes 1048576 | tf_op jit(solution)/shard_map/reshape;squeeze | solution.py:536

commit v5 on v4

--- a/solution.py
+++ b/solution.py
@@ -345,6 +345,8 @@
     first_lane, last_lane = lanes == 0, lanes == 127
     first_sub, last_sub = subs == 0, subs == 7
 
+    gl = g.reshape(1024, 128)
+
     def sweep_row(m, row):
         total = [[None] * 4, [None] * 4]
         for c in range(2):
@@ -361,8 +363,14 @@
         for j in range(4):
             w_re, w_im = w[row, 0, j], w[row, 1, j]
             t_re, t_im = total[0][j], total[1][j]
-            u[m, row, 0, j] = w_re * t_re - w_im * t_im
-            u[m, row, 1, j] = w_re * t_im + w_im * t_re
+            new_re, new_im = w_re * t_re - w_im * t_im, w_re * t_im + w_im * t_re
+            if m < SWEEPS - 1:
+                u[m, row, 0, j] = new_re
+                u[m, row, 1, j] = new_im
+            else:
+                t, r = divmod(row - HALO, 8)
+                gl[pl.ds(j * 32 + t * 16 + r, 8, stride=128), :] = new_re
+                gl[pl.ds(j * 32 + t * 16 + 8 + r, 8, stride=128), :] = new_im
 
     done = [set() for _ in range(SWEEPS)]
 
@@ -396,17 +404,6 @@
         outer_start(0, r, r, fbl)
         outer_start(1, HALO + 24 + r, r, fbl)
     sweeps(0)
-
-    gl = g.reshape(1024, 128)
-
-    def turn_back(r, _):
-        for t in range(2):
-            for j in range(4):
-                for c in range(2):
-                    gl[pl.ds(j * 32 + t * 16 + c * 8 + r, 8, stride=128), :] = u[SWEEPS - 1, HALO + t * 8 + r, c, j]
-        return 0
-
-    lax.fori_loop(0, 8, turn_back, 0)
 
     for half in range(2):
         tiles = [1 - near(cc) if half == 0 else near(cc) for cc in cs]
@@ -517,7 +514,7 @@
             pltpu.VMEM((2,) + planes + (2,) + tile, F32),
             field,
             field,
-            pltpu.VMEM((SWEEPS, ROWS, 2, 4) + tile, F32),
+            pltpu.VMEM((SWEEPS - 1, ROWS, 2, 4) + tile, F32),
             pltpu.VMEM(planes + (2, 2) + tile, F32),
             pltpu.VMEM((2, 32, 2) + tile, F32),
             pltpu.VMEM((2, 2, 32) + tile, F32),

time: 65.3 us -> 65.1 us (level)
  no operation moved by 1% of the time
where the time goes in v5:
time: 65.1 us; the launch traced here: 65 us
  Pallas kernels  62.5 us (96%)
  local copies, waits for them, and re-layouts  1.86 us (3%)
    pallas_call x1, Pallas kernels, body(): pl.pallas_call(kernel, out_shape=jax.ShapeDtypeStruct((2, 2, 2, 16) + til...  62.5 us
    another operation x1, local copies, waits for them, and re-layouts, body(): result[1].reshape(state_rhs.shape)  1.86 us

profile of v5, /device:TPU:1, one launch (start us, length us, event | category | flops | bytes accessed | tf_op | source)
XLA Modules:
  0.0 65.0 jit_solution(16035917119132910001)
XLA Ops:
  0.6 62.5 %precondition.1 = f32[2,2,2,16,8,128]{5,4,3,2,1,0:T(8,128)} custom-call(f32[2,2,16,8,128]{4,3,2,1,0:T(8,128)} %bitcast.7, f32[2,2,16,8,128]{4,3,2,1,0:T(8,128)} %bitcast.8, f32[2,16,8,128]{3,2,1,0:T(8,128)} %bitcast.9), custom_call_target="tpu_custom_call" | custom-call | tf_op jit(solution)/shard_map/precondition/pallas_call | solution.py:499
  63.1 1.9 %slice_bitcast_fusion = (f32[2,2,128,128]{3,2,1,0:T(8,128)}, f32[2,2,128,128]{3,2,1,0:T(8,128)}) fusion(f32[2,2,2,16,8,128]{5,4,3,2,1,0:T(8,128)} %precondition.1), kind=kLoop, calls=%fused_computation | loop fusion | bytes 1048576 | tf_op jit(solution)/shard_map/reshape;squeeze | solution.py:533
